TPU v7x, 32 devices: a whole 2x2x4 slice. The times are simulated.
32 devices in a mesh: gx: 4 (over z), gy: 2 (over y), gz: 4 (over x, core).
Axes of the slice: x: 2, y: 2, z: 4, core: 2. Of those that a mesh axis runs over, the one named last changes fastest.
Arguments:
- displ: float32 [3, 4, 2, 4, 9945], P(None, 'gx', 'gy', 'gz'), may hold values from -6 to 6
- veloc: float32 [3, 4, 2, 4, 9945], P(None, 'gx', 'gy', 'gz'), may hold values from -6 to 6
- accel: float32 [3, 4, 2, 4, 9945], P(None, 'gx', 'gy', 'gz'), may hold values from -12 to 12
- node_index: int32 [4, 2, 4, 125, 128], P('gx', 'gy', 'gz'), may hold values from 0 to 9944, as said below
- inv_map: float32 [4, 2, 4, 9, 125, 128], P('gx', 'gy', 'gz'), may hold values from -1 to 2, as said below
- jac_weight: float32 [4, 2, 4, 125, 128], P('gx', 'gy', 'gz'), may hold values from 0.05 to 0.5
- lame_first: float32 [4, 2, 4, 125, 128], P('gx', 'gy', 'gz'), may hold values from 0.02 to 0.1
- shear_mod: float32 [4, 2, 4, 125, 128], P('gx', 'gy', 'gz'), may hold values from 0.02 to 0.1
- density: float32 [4, 2, 4, 125, 128], P('gx', 'gy', 'gz'), may hold values from 1 to 3
Outputs:
- displ_out: float32 [3, 4, 2, 4, 9945], P(None, 'gx', 'gy', 'gz')
- veloc_out: float32 [3, 4, 2, 4, 9945], P(None, 'gx', 'gy', 'gz')
- accel_out: float32 [3, 4, 2, 4, 9945], P(None, 'gx', 'gy', 'gz')
Inputs may be any that keep to these rules, and one draw needn't show every extreme that they name: `node_index`: on each device the element slots hold the elements of a brick of 4 x 16 x 2 elements in a drawn order, each once; element (ex, ey, ez) has its point (a, b, c) at node ((4 ex + a) * 65 + 4 ey + b) * 9 + 4 ez + c. `inv_map`: the entries with l equal to j are positive.
All inputs are finite; a program needn't handle non-finite values.
Results may differ from a plain program's by a relative error of at most 0.00024.
Values sent between devices are 32-bit elements; how exact they have to be, the bound alone decides.
A program may use at most 64 MiB of HBM per device.

v0:
```python
import jax
import jax.numpy as jnp
import numpy as np
from jax import lax
from jax.experimental import pallas as pl
from jax.experimental.pallas import tpu as pltpu
from jax.sharding import PartitionSpec as P

EX = 4
EY = 16
EZ = 2
NX = 4 * EX + 1
NY = 4 * EY + 1
NZ = 4 * EZ + 1
PLANE = NY * NZ
GROUP = 4
GROUPS = EY // GROUP
STEP = 4 * GROUP * NZ
SPAN = 256
WIDE = 640
GROW = 64
SROW = 72
SUB = EZ * GROUP

LIMIT = 65 * 1000 * 1000

time_step = 0.1
MESH = pl.DeviceIdType.MESH


def derivative_table():
    points = np.array([-1.0, -np.sqrt(3.0 / 7.0), 0.0, np.sqrt(3.0 / 7.0), 1.0])
    count = points.shape[0]
    weights = np.array(
        [
            1.0 / np.prod([points[s] - points[o] for o in range(count) if o != s])
            for s in range(count)
        ]
    )
    table = np.zeros((count, count))
    for t in range(count):
        for s in range(count):
            if t != s:
                table[t, s] = weights[s] / weights[t] / (points[t] - points[s])
        table[t, t] = -np.sum(table[t])
    return table


def constants():
    table = derivative_table()
    select = np.zeros((25 * SUB, SPAN), np.float32)
    for b in range(5):
        for c in range(5):
            for ez in range(EZ):
                for ey in range(GROUP):
                    row = (b * 5 + c) * SUB + ez * GROUP + ey
                    select[row, (4 * ey + b) * NZ + 4 * ez + c] = 1.0
    eye = np.eye(5)
    parts = [
        np.kron(table, np.kron(eye, eye)),
        np.kron(eye, np.kron(table, eye)),
        np.kron(eye, np.kron(eye, table)),
    ]
    pad = np.zeros((125, 160))
    for a in range(5):
        for q in range(25):
            pad[a * 25 + q, a * 32 + q] = 1.0
    deriv = np.zeros((384, 160), np.float32)
    for l in range(3):
        deriv[l * 128 : l * 128 + 125] = parts[l] @ pad
    spread = np.zeros((160, 128), np.float32)
    spread[:, :125] = pad.T
    return select, deriv, -deriv.T.copy(), spread


def split2(x):
    hi = x.astype(jnp.bfloat16)
    low = (x - hi.astype(jnp.float32)).astype(jnp.bfloat16)
    return (hi, low)


def halves(x):
    hi = np.asarray(x, jnp.bfloat16)
    low = np.asarray(x - hi.astype(np.float32), jnp.bfloat16)
    return np.stack([hi, low])


def product(pair, y):
    hi, low = split2(y)
    dot = lambda a, b: jnp.dot(a, b, preferred_element_type=jnp.float32)
    return dot(pair[0], hi) + dot(pair[0], low) + dot(pair[1], hi)


def dots(x, y, dims, split_left):
    total = None
    for piece in split2(x if split_left else y):
        left, right = (piece, y) if split_left else (x, piece)
        out = lax.dot_general(
            left, right, (dims, ((), ())), preferred_element_type=jnp.float32
        )
        total = out if total is None else total + out
    return total


def squeezed(ref):
    return ref.at[:, 0] if len(ref.shape) == 3 else ref.at[:, :, 0]


def kernel(
    displ, veloc, accel, node, inv, jac, lame, shear, dens,
    select_ref, deriv_ref, back_ref, spread_ref,
    pos_out, vel_out, acc_out,
    select_s, deriv_s, back_s, spread_s,
    d_s, v_s, a_s, node_s, inv_s, jac_s, lame_s, shear_s, dens_s,
    nf, u_s, fl_s, md_s, zp_s, grid_s,
    z_send, z_recv, y_send, y_recv, x_send, x_recv,
    in_sem, send_sem, recv_sem,
):
    names = ("gz", "gy", "gx")
    spots = [lax.axis_index(n) for n in names]
    sizes = [lax.axis_size(n) for n in names]
    has_low = [s > 0 for s in spots]
    has_high = [s < n - 1 for s, n in zip(spots, sizes)]
    barrier = pltpu.get_barrier_semaphore()
    for n, s, lo, hi in zip(names, spots, has_low, has_high):

        @pl.when(lo)
        def _():
            pl.semaphore_signal(barrier, inc=1, device_id={n: s - 1}, device_id_type=MESH)

        @pl.when(hi)
        def _():
            pl.semaphore_signal(barrier, inc=1, device_id={n: s + 1}, device_id_type=MESH)

    copies = []
    for k, (src, dst) in enumerate(((displ, d_s), (veloc, v_s), (accel, a_s))):
        for c in range(3):
            copies.append(
                pltpu.make_async_copy(
                    src.at[c], dst.at[pl.ds(c, 1)], in_sem.at[3 * k + c]
                )
            )
    elems = ((node, node_s), (inv, inv_s), (jac, jac_s), (lame, lame_s), (shear, shear_s), (dens, dens_s))
    for k, (src, dst) in enumerate(elems):
        copies.append(pltpu.make_async_copy(squeezed(src), dst, in_sem.at[9 + k]))
    consts = ((select_ref, select_s), (deriv_ref, deriv_s), (back_ref, back_s), (spread_ref, spread_s))
    for k, (src, dst) in enumerate(consts):
        copies.append(pltpu.make_async_copy(src, dst, in_sem.at[15 + k]))
    for cp in copies:
        cp.start()
    nf[...] = jnp.zeros_like(nf)
    u_s[...] = jnp.zeros_like(u_s)
    fl_s[...] = jnp.zeros_like(fl_s)
    md_s[...] = jnp.zeros_like(md_s)
    for cp in copies[:10] + copies[15:16]:
        cp.wait()

    half = 0.5 * time_step
    pos = d_s[...] + time_step * v_s[...] + (half * time_step) * a_s[...]
    d_s[...] = pos
    vel_out[...] = v_s[...] + half * a_s[...]
    pos_out[...] = pos
    for x in range(NX):
        nf[3 * x : 3 * x + 3, 0:PLANE] = d_s[:, PLANE * x : PLANE * (x + 1)]
    planes = nf[...]
    blocks = [planes[:, :SPAN]] + [
        pltpu.roll(planes, WIDE - STEP * g, 1)[:, :SPAN] for g in range(1, GROUPS)
    ]
    rows = jnp.concatenate(blocks, axis=0)
    select = select_s[...]
    lifted = dots(select, rows, ((1,), (1,)), False)

    corner = node_s[0:1, :].astype(jnp.float32)
    x0 = jnp.floor((corner + 0.5) * (1.0 / PLANE))
    rem = corner - PLANE * x0
    y0 = jnp.floor((rem + 0.5) * (1.0 / NZ))
    z0 = rem - NZ * y0
    grp = jnp.floor((y0 + 0.5) * (1.0 / (4 * GROUP)))
    low = (y0 - 4 * GROUP * grp) * 0.25 + GROUP * (z0 * 0.25)
    sub = lax.broadcasted_iota(jnp.int32, (SUB, 128), 0).astype(jnp.float32)
    mask = jnp.where(sub == low, 1.0, 0.0)[None]

    iota = lax.broadcasted_iota(jnp.int32, (GROUPS * GROW, 128), 0).astype(jnp.float32)
    goal = grp * GROW + 3.0 * x0
    picks = jnp.concatenate(
        [
            jnp.where(iota == goal + (3.0 * a + c), 1.0, 0.0).astype(jnp.bfloat16)
            for c in range(3)
            for a in range(5)
        ],
        axis=1,
    )
    gathered = dots(lifted, picks, ((1,), (0,)), True)
    for c in range(3):
        for a in range(5):
            j = (c * 5 + a) * 128
            part = gathered[:, j : j + 128].reshape(25, SUB, 128) * mask
            u_s[a * 32 : a * 32 + 25, c * 128 : (c + 1) * 128] = jnp.sum(part, axis=1)

    for cp in copies[16:]:
        cp.wait()
    local = product(deriv_s, u_s[...])
    for cp in copies[10:15]:
        cp.wait()
    grads = [
        [local[l * 128 : l * 128 + 125, c * 128 : (c + 1) * 128] for c in range(3)]
        for l in range(3)
    ]
    maps = [[inv_s[3 * l + j] for j in range(3)] for l in range(3)]
    weight = jac_s[...]
    lam = lame_s[...]
    mu = shear_s[...]
    h = [
        [sum(grads[l][c] * maps[l][j] for l in range(3)) for j in range(3)] for c in range(3)
    ]
    div = lam * (h[0][0] + h[1][1] + h[2][2])
    stress = [[None] * 3 for _ in range(3)]
    for c in range(3):
        for j in range(c, 3):
            s = mu * (h[c][j] + h[j][c])
            if c == j:
                s = s + div
            s = s * weight
            stress[c][j] = s
            stress[j][c] = s
    for l in range(3):
        for c in range(3):
            fl_s[l * 128 : l * 128 + 125, c * 128 : (c + 1) * 128] = sum(
                stress[c][j] * maps[l][j] for j in range(3)
            )
    md_s[0:125, :] = dens_s[...] * weight
    terms = product(back_s, fl_s[...])
    heavy = sum(
        jnp.dot(spread_s[...], part, preferred_element_type=jnp.float32)
        for part in split2(md_s[...])
    )

    spread_out = []
    puts = []
    iota2 = lax.broadcasted_iota(jnp.int32, (GROUPS * SROW, 128), 0).astype(jnp.float32)
    goal2 = grp * SROW + 4.0 * x0
    for k in range(4):
        for a in range(5):
            part = terms[a * 32 : a * 32 + 25, k * 128 : (k + 1) * 128] if k < 3 else heavy[a * 32 : a * 32 + 25]
            spread_out.append((part[:, None, :] * mask).reshape(25 * SUB, 128))
            puts.append(
                jnp.where(iota2 == goal2 + (4.0 * a + k), 1.0, 0.0).astype(jnp.bfloat16)
            )
    zp_s[...] = dots(
        jnp.concatenate(spread_out, axis=1),
        jnp.concatenate(puts, axis=1),
        ((1,), (1,)),
        True,
    )

    peers = sum(flag.astype(jnp.int32) for flag in has_low + has_high)
    pl.semaphore_wait(barrier, peers)

    def exchange(axis, send, recv):
        name, spot = names[axis], spots[axis]

        def copy(side, peer):
            return pltpu.make_async_remote_copy(
                src_ref=send.at[side],
                dst_ref=recv.at[1 - side],
                send_sem=send_sem.at[2 * axis + side],
                recv_sem=recv_sem.at[2 * axis + 1 - side],
                device_id={name: peer},
                device_id_type=MESH,
            )

        @pl.when(has_low[axis])
        def _():
            copy(0, spot - 1).start()

        @pl.when(has_high[axis])
        def _():
            copy(1, spot + 1).start()

        def finish(side):
            copy(1 - side, spot).wait_recv()

        def drain():
            for side, ok in ((0, has_low[axis]), (1, has_high[axis])):

                @pl.when(ok)
                def _():
                    copy(side, spot).wait_send()

        return finish, drain

    drains = []
    for b in range(5):
        z_send[0, b * 4 : b * 4 + 4] = zp_s[b * 5 * SUB : b * 5 * SUB + GROUP]
        top = (b * 5 + 4) * SUB + (EZ - 1) * GROUP
        z_send[1, b * 4 : b * 4 + 4] = zp_s[top : top + GROUP]
    finish, drain = exchange(0, z_send, z_recv)
    drains.append(drain)

    @pl.when(has_low[0])
    def _():
        finish(0)
        for b in range(5):
            at = b * 5 * SUB
            zp_s[at : at + GROUP] += z_recv[0, b * 4 : b * 4 + 4]

    @pl.when(has_high[0])
    def _():
        finish(1)
        for b in range(5):
            at = (b * 5 + 4) * SUB + (EZ - 1) * GROUP
            zp_s[at : at + GROUP] += z_recv[1, b * 4 : b * 4 + 4]

    flat = dots(zp_s[...], select, ((0,), (0,)), True)
    total = None
    blank = jnp.zeros((SROW, WIDE - SPAN), jnp.float32)
    for g in range(GROUPS):
        piece = jnp.concatenate([flat[g * SROW : (g + 1) * SROW], blank], axis=1)
        if g:
            piece = pltpu.roll(piece, STEP * g, 1)
        total = piece if total is None else total + piece
    grid_s[...] = total

    edge = WIDE - 128
    shift = PLANE - NZ - edge
    lanes = lax.broadcasted_iota(jnp.int32, (SROW, 128), 1)
    y_send[0] = grid_s[:, 0:128]
    y_send[1] = grid_s[:, edge:WIDE]
    finish, drain = exchange(1, y_send, y_recv)
    drains.append(drain)

    @pl.when(has_low[1])
    def _():
        finish(0)
        got = pltpu.roll(y_recv[0], 128 - shift, 1)
        grid_s[:, 0:128] += jnp.where(lanes < NZ, got, 0.0)

    @pl.when(has_high[1])
    def _():
        finish(1)
        got = jnp.where(lanes < NZ, y_recv[1], 0.0)
        grid_s[:, edge:WIDE] += pltpu.roll(got, shift, 1)

    x_send[0] = grid_s[0:8]
    x_send[1] = grid_s[SROW - 8 : SROW]
    finish, drain = exchange(2, x_send, x_recv)
    drains.append(drain)

    @pl.when(has_low[2])
    def _():
        finish(0)
        grid_s[0:4] += x_recv[0, 0:4]

    @pl.when(has_high[2])
    def _():
        finish(1)
        grid_s[SROW - 8 : SROW - 4] += x_recv[1, 0:4]

    for x in range(NX):
        force = grid_s[4 * x : 4 * x + 3, 0:PLANE]
        mass = grid_s[4 * x + 3 : 4 * x + 4, 0:PLANE]
        acc_out[:, PLANE * x : PLANE * (x + 1)] = force / mass
    for drain in drains:
        drain()


def finish(pos, vel, acc, pos_out, vel_out, acc_out, v_s, sem):
    def put(src, dst, k):
        copies = [
            pltpu.make_async_copy(src.at[pl.ds(c, 1)], dst.at[c], sem.at[k + c]) for c in range(3)
        ]
        for cp in copies:
            cp.start()
        return copies

    copies = put(pos, pos_out, 0) + put(acc, acc_out, 3)
    v_s[...] = vel[...] + (0.5 * time_step) * acc[...]
    for cp in copies + put(v_s, vel_out, 6):
        cp.wait()


def body(displ, veloc, accel, node_index, inv_map, jac_weight, lame_first, shear_mod, density):
    nodes = displ.shape[4]
    elements = node_index.shape[4]
    select, deriv, back, spread = constants()
    deriv, back = halves(deriv), halves(back)
    fields = [x.reshape(3, 1, nodes) for x in (displ, veloc, accel)]
    elems = [
        x.reshape(125, 1, elements) for x in (jac_weight, lame_first, shear_mod, density)
    ]
    vmem = pl.BlockSpec(memory_space=pltpu.VMEM)
    hbm = pl.BlockSpec(memory_space=pltpu.HBM)
    f32 = jnp.float32
    out = jax.ShapeDtypeStruct((3, 1, nodes), f32)
    elem = pltpu.VMEM((125, elements), f32)
    width = GROUPS * SROW
    result = pl.pallas_call(
        kernel,
        out_shape=[pltpu.VMEM((3, nodes), f32)] * 3,
        in_specs=[hbm] * 13,
        out_specs=[vmem] * 3,
        scratch_shapes=[
            pltpu.VMEM(select.shape, jnp.bfloat16),
            pltpu.VMEM(deriv.shape, jnp.bfloat16),
            pltpu.VMEM(back.shape, jnp.bfloat16),
            pltpu.VMEM(spread.shape, jnp.bfloat16),
            pltpu.VMEM((3, nodes), f32),
            pltpu.VMEM((3, nodes), f32),
            pltpu.VMEM((3, nodes), f32),
            pltpu.VMEM((125, elements), jnp.int32),
            pltpu.VMEM((9, 125, elements), f32),
            elem, elem, elem, elem,
            pltpu.VMEM((GROW, WIDE), f32),
            pltpu.VMEM((160, 384), f32),
            pltpu.VMEM((384, 384), f32),
            pltpu.VMEM((128, 128), f32),
            pltpu.VMEM((25 * SUB, width), f32),
            pltpu.VMEM((SROW, WIDE), f32),
            pltpu.VMEM((2, 24, width), f32),
            pltpu.VMEM((2, 24, width), f32),
            pltpu.VMEM((2, SROW, 128), f32),
            pltpu.VMEM((2, SROW, 128), f32),
            pltpu.VMEM((2, 8, WIDE), f32),
            pltpu.VMEM((2, 8, WIDE), f32),
            pltpu.SemaphoreType.DMA((19,)),
            pltpu.SemaphoreType.DMA((6,)),
            pltpu.SemaphoreType.DMA((6,)),
        ],
        compiler_params=pltpu.CompilerParams(
            collective_id=0, has_side_effects=True, vmem_limit_bytes=LIMIT
        ),
    )(
        *fields,
        node_index.reshape(125, 1, elements),
        inv_map.reshape(9, 125, 1, elements),
        *elems,
        jnp.asarray(select, jnp.bfloat16),
        jnp.asarray(deriv),
        jnp.asarray(back),
        jnp.asarray(spread, jnp.bfloat16),
    )
    final = pl.pallas_call(
        finish,
        out_shape=[out] * 3,
        in_specs=[vmem] * 3,
        out_specs=[hbm] * 3,
        scratch_shapes=[pltpu.VMEM((3, nodes), f32), pltpu.SemaphoreType.DMA((9,))],
        compiler_params=pltpu.CompilerParams(vmem_limit_bytes=LIMIT),
    )(*[pltpu.with_memory_space_constraint(x, pltpu.VMEM) for x in result])
    return tuple(x.reshape(displ.shape) for x in final)


def solution(mesh):
    field = P(None, "gx", "gy", "gz", None)
    elem = P("gx", "gy", "gz", None, None)
    placed = (field,) * 3 + (elem, P("gx", "gy", "gz", None, None, None)) + (elem,) * 4
    return jax.shard_map(
        body, mesh=mesh, in_specs=placed, out_specs=(field,) * 3, check_vma=False
    )
```

profile of v0, /device:TPU:1, one launch (start us, length us, event | category | flops | bytes accessed | tf_op | source)
XLA Modules:
  0.0 17.7 jit_solution(9282301069968811883)
XLA Ops:
  0.6 16.3 %shard_map.148 = (f32[3,9945]{1,0:T(4,128)S(1)}, f32[3,9945]{1,0:T(4,128)S(1)}, f32[3,9945]{1,0:T(4,128)S(1)}) custom-call(f32[3,1,9945]{2,1,0:T(1,128)} %bitcast.19, f32[3,1,9945]{2,1,0:T(1,128)} %bitcast.20, f32[3,1,9945]{2,1,0:T(1,128)} %bitcast.21, s32[125,1,128]{2,1,0:T(1,128)} %bitcast.22, f32[9,125,1,128]{3,2,1,0:T(1,128)} %bitcast.18, ...), custom_call_target="tpu_custom_call" | custom-call | tf_op jit(solution)/shard_map/pallas_call | solution.py:397
  16.9 0.8 %shard_map.149 = (f32[3,1,9945]{2,1,0:T(1,128)}, f32[3,1,9945]{2,1,0:T(1,128)}, f32[3,1,9945]{2,1,0:T(1,128)}) custom-call(f32[3,9945]{1,0:T(4,128)S(1)} %get-tuple-element.9.pos, f32[3,9945]{1,0:T(4,128)S(1)} %get-tuple-element.10.vel, f32[3,9945]{1,0:T(4,128)S(1)} %get-tuple-element.11.acc), custom_call_target="tpu_custom_call" | custom-call | tf_op jit(solution)/shard_map/pallas_call | solution.py:442
where the time goes:
time: 17.9 us; the launch traced here: 17.7 us
  Pallas kernels  17.1 us (96%)
  between operations  0.64 us (4%)
    pallas_call x1, Pallas kernels, body(): pl.pallas_call(kernel, out_shape=[pltpu.VMEM((3, nodes), f32)] * 3, in_sp...  16.3 us
    pallas_call x1, Pallas kernels, body(): pl.pallas_call(finish, out_shape=[out] * 3, in_specs=[vmem] * 3, out_spec...  0.8 us

commit v1 on v0

--- a/solution.py
+++ b/solution.py
@@ -21,6 +21,11 @@
 GROW = 64
 SROW = 72
 SUB = EZ * GROUP
+REACH = (4 * GROUP + 1) * NZ
+FACE = 160
+EDGE = 512
+TAIL = PLANE - NZ - EDGE
+PITCH = 14
 
 LIMIT = 65 * 1000 * 1000
 
@@ -55,6 +60,10 @@
                 for ey in range(GROUP):
                     row = (b * 5 + c) * SUB + ez * GROUP + ey
                     select[row, (4 * ey + b) * NZ + 4 * ez + c] = 1.0
+                    if ez == 0 and c == 0:
+                        select[row, FACE + 4 * ey + b] = 1.0
+                    if ez == EZ - 1 and c == 4:
+                        select[row, FACE + 32 + 4 * ey + b] = 1.0
     eye = np.eye(5)
     parts = [
         np.kron(table, np.kron(eye, eye)),
@@ -102,6 +111,35 @@
     return total
 
 
+def ways():
+    steps = (0, -1, 1)
+    found = [(x, y, z) for z in steps for y in steps for x in steps][1:]
+    half = [w for w in found if w > (0, 0, 0)]
+    half.sort(key=lambda w: (sum(map(abs, w)), -abs(w[2])))
+    other = [tuple(-v for v in w) for w in half]
+    return half + other[::-1]
+
+
+WAYS = ways()
+
+
+def neighbours():
+    names = ("gx", "gy", "gz")
+    spots = [lax.axis_index(n) for n in names]
+    sizes = [lax.axis_size(n) for n in names]
+    links = []
+    for way in WAYS:
+        there = None
+        peer = {}
+        for n, s, z, w in zip(names, spots, sizes, way):
+            if w:
+                ok = s > 0 if w < 0 else s < z - 1
+                there = ok if there is None else there & ok
+                peer[n] = s + w
+        links.append((way, there, peer))
+    return links
+
+
 def squeezed(ref):
     return ref.at[:, 0] if len(ref.shape) == 3 else ref.at[:, :, 0]
 
@@ -112,26 +150,12 @@
     pos_out, vel_out, acc_out,
     select_s, deriv_s, back_s, spread_s,
     d_s, v_s, a_s, node_s, inv_s, jac_s, lame_s, shear_s, dens_s,
-    nf, u_s, fl_s, md_s, zp_s, grid_s,
-    z_send, z_recv, y_send, y_recv, x_send, x_recv,
+    nf, u_s, fl_s, md_s, grid_s,
+    m_send, p_send, x_send, e_send,
+    m_recv, p_recv, q_recv, x_recv, e_recv, f_recv, c_recv,
     in_sem, send_sem, recv_sem,
 ):
-    names = ("gz", "gy", "gx")
-    spots = [lax.axis_index(n) for n in names]
-    sizes = [lax.axis_size(n) for n in names]
-    has_low = [s > 0 for s in spots]
-    has_high = [s < n - 1 for s, n in zip(spots, sizes)]
-    barrier = pltpu.get_barrier_semaphore()
-    for n, s, lo, hi in zip(names, spots, has_low, has_high):
-
-        @pl.when(lo)
-        def _():
-            pl.semaphore_signal(barrier, inc=1, device_id={n: s - 1}, device_id_type=MESH)
-
-        @pl.when(hi)
-        def _():
-            pl.semaphore_signal(barrier, inc=1, device_id={n: s + 1}, device_id_type=MESH)
-
+    links = neighbours()
     copies = []
     for k, (src, dst) in enumerate(((displ, d_s), (veloc, v_s), (accel, a_s))):
         for c in range(3):
@@ -152,6 +176,15 @@
     u_s[...] = jnp.zeros_like(u_s)
     fl_s[...] = jnp.zeros_like(fl_s)
     md_s[...] = jnp.zeros_like(md_s)
+    for ref in (m_recv, p_recv, q_recv, x_recv, e_recv, f_recv, c_recv):
+        ref[...] = jnp.zeros_like(ref)
+    barrier = pltpu.get_barrier_semaphore()
+    for way, there, peer in links:
+
+        @pl.when(there)
+        def _():
+            pl.semaphore_signal(barrier, inc=1, device_id=peer, device_id_type=MESH)
+
     for cp in copies[:10] + copies[15:16]:
         cp.wait()
 
@@ -167,6 +200,8 @@
         pltpu.roll(planes, WIDE - STEP * g, 1)[:, :SPAN] for g in range(1, GROUPS)
     ]
     rows = jnp.concatenate(blocks, axis=0)
+    inside = lax.broadcasted_iota(jnp.int32, (1, SPAN), 1) < REACH
+    rows = jnp.where(inside, rows, 0.0)
     select = select_s[...]
     lifted = dots(select, rows, ((1,), (1,)), False)
 
@@ -246,122 +281,155 @@
             puts.append(
                 jnp.where(iota2 == goal2 + (4.0 * a + k), 1.0, 0.0).astype(jnp.bfloat16)
             )
-    zp_s[...] = dots(
-        jnp.concatenate(spread_out, axis=1),
-        jnp.concatenate(puts, axis=1),
-        ((1,), (1,)),
-        True,
-    )
-
-    peers = sum(flag.astype(jnp.int32) for flag in has_low + has_high)
-    pl.semaphore_wait(barrier, peers)
-
-    def exchange(axis, send, recv):
-        name, spot = names[axis], spots[axis]
-
-        def copy(side, peer):
-            return pltpu.make_async_remote_copy(
-                src_ref=send.at[side],
-                dst_ref=recv.at[1 - side],
-                send_sem=send_sem.at[2 * axis + side],
-                recv_sem=recv_sem.at[2 * axis + 1 - side],
-                device_id={name: peer},
-                device_id_type=MESH,
-            )
-
-        @pl.when(has_low[axis])
-        def _():
-            copy(0, spot - 1).start()
-
-        @pl.when(has_high[axis])
-        def _():
-            copy(1, spot + 1).start()
-
-        def finish(side):
-            copy(1 - side, spot).wait_recv()
-
-        def drain():
-            for side, ok in ((0, has_low[axis]), (1, has_high[axis])):
-
-                @pl.when(ok)
-                def _():
-                    copy(side, spot).wait_send()
-
-        return finish, drain
-
-    drains = []
-    for b in range(5):
-        z_send[0, b * 4 : b * 4 + 4] = zp_s[b * 5 * SUB : b * 5 * SUB + GROUP]
-        top = (b * 5 + 4) * SUB + (EZ - 1) * GROUP
-        z_send[1, b * 4 : b * 4 + 4] = zp_s[top : top + GROUP]
-    finish, drain = exchange(0, z_send, z_recv)
-    drains.append(drain)
-
-    @pl.when(has_low[0])
-    def _():
-        finish(0)
-        for b in range(5):
-            at = b * 5 * SUB
-            zp_s[at : at + GROUP] += z_recv[0, b * 4 : b * 4 + 4]
-
-    @pl.when(has_high[0])
-    def _():
-        finish(1)
-        for b in range(5):
-            at = (b * 5 + 4) * SUB + (EZ - 1) * GROUP
-            zp_s[at : at + GROUP] += z_recv[1, b * 4 : b * 4 + 4]
-
-    flat = dots(zp_s[...], select, ((0,), (0,)), True)
+    puts_all = jnp.concatenate(puts, axis=1)
+    zp = dots(jnp.concatenate(spread_out, axis=1), puts_all, ((1,), (1,)), True)
+
+    flat = dots(zp, select, ((0,), (0,)), True)
+    lanes = lax.broadcasted_iota(jnp.int32, (SROW, 128), 1)
+    wide = lax.broadcasted_iota(jnp.int32, (1, SPAN), 1)
     total = None
+    faces = [None, None]
     blank = jnp.zeros((SROW, WIDE - SPAN), jnp.float32)
     for g in range(GROUPS):
-        piece = jnp.concatenate([flat[g * SROW : (g + 1) * SROW], blank], axis=1)
+        piece = flat[g * SROW : (g + 1) * SROW]
+        for side in range(2):
+            at = FACE - 128 + 32 * side
+            face = pltpu.roll(piece[:, 128:], (4 * GROUP * g - at) % 128, 1)
+            first = 4 * GROUP * g
+            face = jnp.where((lanes >= first) & (lanes <= first + 4 * GROUP), face, 0.0)
+            faces[side] = face if g == 0 else faces[side] + face
+        piece = jnp.concatenate([jnp.where(wide < REACH, piece, 0.0), blank], axis=1)
         if g:
             piece = pltpu.roll(piece, STEP * g, 1)
         total = piece if total is None else total + piece
+
     grid_s[...] = total
-
-    edge = WIDE - 128
-    shift = PLANE - NZ - edge
-    lanes = lax.broadcasted_iota(jnp.int32, (SROW, 128), 1)
-    y_send[0] = grid_s[:, 0:128]
-    y_send[1] = grid_s[:, edge:WIDE]
-    finish, drain = exchange(1, y_send, y_recv)
-    drains.append(drain)
-
-    @pl.when(has_low[1])
-    def _():
-        finish(0)
-        got = pltpu.roll(y_recv[0], 128 - shift, 1)
-        grid_s[:, 0:128] += jnp.where(lanes < NZ, got, 0.0)
-
-    @pl.when(has_high[1])
-    def _():
-        finish(1)
-        got = jnp.where(lanes < NZ, y_recv[1], 0.0)
-        grid_s[:, edge:WIDE] += pltpu.roll(got, shift, 1)
-
-    x_send[0] = grid_s[0:8]
-    x_send[1] = grid_s[SROW - 8 : SROW]
-    finish, drain = exchange(2, x_send, x_recv)
-    drains.append(drain)
-
-    @pl.when(has_low[2])
-    def _():
-        finish(0)
-        grid_s[0:4] += x_recv[0, 0:4]
-
-    @pl.when(has_high[2])
-    def _():
-        finish(1)
-        grid_s[SROW - 8 : SROW - 4] += x_recv[1, 0:4]
+    ends = (total[:, 0:128], pltpu.roll(total[:, EDGE:WIDE], 128 - TAIL, 1))
+    rows8 = [slice(8 * i, 8 * i + 8) for i in range(SROW // 8)]
+    lane8 = lax.broadcasted_iota(jnp.int32, (8, 128), 1)
+    for side in range(2):
+        m_send[side] = faces[side]
+        top = 4 * (NX - 1) * side
+        x_send[side] = total[top : top + 4]
+        for dz in range(2):
+            e_send[side, dz] = faces[dz][top : top + 4]
+        packed = None
+        for i, part in enumerate(rows8):
+            got = jnp.where(lane8 < NZ, ends[side][part], 0.0)
+            got = pltpu.roll(got, PITCH * i, 1) if i else got
+            packed = got if packed is None else packed + got
+        p_send[side] = packed
+
+    def copy(k, way, peer, arriving):
+        ref_from, ref_to = route(way, arriving)
+        return pltpu.make_async_remote_copy(
+            src_ref=ref_from,
+            dst_ref=ref_to,
+            send_sem=send_sem.at[k],
+            recv_sem=recv_sem.at[len(WAYS) - 1 - k if not arriving else k],
+            device_id=peer,
+            device_id_type=MESH,
+        )
+
+    def route(way, arriving):
+        low = tuple((w + 1) // 2 for w in way)
+        sx, sy, sz = low
+        if arriving:
+            ox, oy, oz = low
+            sx, sy, sz = 1 - sx, 1 - sy, 1 - sz
+        else:
+            ox, oy, oz = 1 - sx, 1 - sy, 1 - sz
+        dx, dy, dz = (w != 0 for w in way)
+        end = pl.ds(EDGE * sy, 128)
+        if dx and dy and dz:
+            return x_send.at[sx, :, end], c_recv.at[ox, oy, oz]
+        if dx and dy:
+            return x_send.at[sx, :, end], f_recv.at[ox, oy]
+        if dx and dz:
+            return e_send.at[sx, sz], e_recv.at[ox, oz]
+        if dy and dz:
+            return p_send.at[sy], q_recv.at[oy, oz]
+        if dx:
+            return x_send.at[sx], x_recv.at[ox]
+        if dy:
+            return p_send.at[sy], p_recv.at[oy]
+        return m_send.at[sz], m_recv.at[oz]
+
+    peers = sum(there.astype(jnp.int32) for way, there, peer in links)
+    pl.semaphore_wait(barrier, peers)
+    farthest = sorted(range(len(WAYS)), key=lambda k: -sum(map(abs, WAYS[k])))
+    for k in farthest:
+        way, there, peer = links[k]
+
+        @pl.when(there)
+        def _():
+            copy(k, way, peer, False).start()
+
+    for k, (way, there, peer) in enumerate(links):
+
+        @pl.when(there)
+        def _():
+            copy(k, way, peer, True).wait_recv()
+
+    full = []
+    pad = jnp.zeros((SROW - 4 * NX, 128), jnp.float32)
+    gap = jnp.zeros((4 * NX - 8, 128), jnp.float32)
+    for dz in range(2):
+        rim = jnp.concatenate([e_recv[0, dz], gap, e_recv[1, dz], pad], axis=0)
+        full.append(m_recv[dz] + rim)
+    strips = []
+    for sy in range(2):
+        sums = p_recv[sy]
+        for dz in range(2):
+            got = pltpu.roll(q_recv[sy, dz], 128 - 8 if dz == 0 else 8, 1)
+            here = lax.rem(lane8, PITCH) == (NZ - 1) * dz
+            sums = sums + jnp.where(here & (lane8 < PITCH * 9), got, 0.0)
+        parts = []
+        for i in range(SROW // 8):
+            got = pltpu.roll(sums, 128 - PITCH * i, 1) if i else sums
+            parts.append(jnp.where(lane8 < NZ, got, 0.0))
+        strip = jnp.concatenate(parts, axis=0)
+        corners = []
+        for sx in range(2):
+            shift = 128 - TAIL if sy == 0 else 0
+            got = f_recv[sx, sy]
+            got = pltpu.roll(got, shift, 1) if shift else got
+            lane4 = lax.broadcasted_iota(jnp.int32, (4, 128), 1)
+            got = jnp.where(lane4 < NZ, got, 0.0)
+            for dz in range(2):
+                far = c_recv[sx, sy, dz]
+                far = pltpu.roll(far, (shift + (128 - 8 if dz == 0 else 8)) % 128, 1)
+                got = got + jnp.where(lane4 == (NZ - 1) * dz, far, 0.0)
+            corners.append(got)
+        strip = strip + jnp.concatenate([corners[0], gap, corners[1], pad], axis=0)
+        strips.append(strip if sy == 0 else pltpu.roll(strip, TAIL, 1))
+    for j in range(WIDE // 128):
+        at = slice(128 * j, 128 * j + 128)
+        node = lanes + 128 * j
+        along = lax.div(node, NZ)
+        depth = node - NZ * along
+        sums = grid_s[:, at]
+        for dz in range(2):
+            got = jnp.take_along_axis(full[dz], jnp.minimum(along, 127), axis=1)
+            sums = sums + jnp.where((depth == (NZ - 1) * dz) & (along < NY), got, 0.0)
+        if j == 0:
+            sums = sums + strips[0]
+        if j == WIDE // 128 - 1:
+            sums = sums + strips[1]
+        grid_s[:, at] = sums
+        for sx in range(2):
+            top = 4 * (NX - 1) * sx
+            grid_s[top : top + 4, at] += x_recv[sx, :, at]
 
     for x in range(NX):
         force = grid_s[4 * x : 4 * x + 3, 0:PLANE]
         mass = grid_s[4 * x + 3 : 4 * x + 4, 0:PLANE]
         acc_out[:, PLANE * x : PLANE * (x + 1)] = force / mass
-    for drain in drains:
-        drain()
+    for k, (way, there, peer) in enumerate(links):
+
+        @pl.when(there)
+        def _():
+            copy(k, way, peer, False).wait_send()
 
 
 def finish(pos, vel, acc, pos_out, vel_out, acc_out, v_s, sem):
@@ -393,7 +461,6 @@
     f32 = jnp.float32
     out = jax.ShapeDtypeStruct((3, 1, nodes), f32)
     elem = pltpu.VMEM((125, elements), f32)
-    width = GROUPS * SROW
     result = pl.pallas_call(
         kernel,
         out_shape=[pltpu.VMEM((3, nodes), f32)] * 3,
@@ -414,17 +481,21 @@
             pltpu.VMEM((160, 384), f32),
             pltpu.VMEM((384, 384), f32),
             pltpu.VMEM((128, 128), f32),
-            pltpu.VMEM((25 * SUB, width), f32),
             pltpu.VMEM((SROW, WIDE), f32),
-            pltpu.VMEM((2, 24, width), f32),
-            pltpu.VMEM((2, 24, width), f32),
             pltpu.VMEM((2, SROW, 128), f32),
+            pltpu.VMEM((2, 8, 128), f32),
+            pltpu.VMEM((2, 4, WIDE), f32),
+            pltpu.VMEM((2, 2, 4, 128), f32),
             pltpu.VMEM((2, SROW, 128), f32),
-            pltpu.VMEM((2, 8, WIDE), f32),
-            pltpu.VMEM((2, 8, WIDE), f32),
+            pltpu.VMEM((2, 8, 128), f32),
+            pltpu.VMEM((2, 2, 8, 128), f32),
+            pltpu.VMEM((2, 4, WIDE), f32),
+            pltpu.VMEM((2, 2, 4, 128), f32),
+            pltpu.VMEM((2, 2, 4, 128), f32),
+            pltpu.VMEM((2, 2, 2, 4, 128), f32),
             pltpu.SemaphoreType.DMA((19,)),
-            pltpu.SemaphoreType.DMA((6,)),
-            pltpu.SemaphoreType.DMA((6,)),
+            pltpu.SemaphoreType.DMA((26,)),
+            pltpu.SemaphoreType.DMA((26,)),
         ],
         compiler_params=pltpu.CompilerParams(
             collective_id=0, has_side_effects=True, vmem_limit_bytes=LIMIT

time: 17.9 us -> 14.5 us (0.81)
  Pallas kernels: 17.1 us -> 13.7 us
    pallas_call x1, Pallas kernels: 16.3 us -> 12.9 us  [body(): pl.pallas_call(kernel, out_shape=[pltpu.VMEM((3, nodes), f32)] * 3, in_sp...]
where the time goes in v1:
time: 14.5 us; the launch traced here: 14.3 us
  Pallas kernels  13.7 us (94%)
  between operations  0.64 us (4%)
    pallas_call x1, Pallas kernels, body(): pl.pallas_call(kernel, out_shape=[pltpu.VMEM((3, nodes), f32)] * 3, in_sp...  12.9 us
    pallas_call x1, Pallas kernels, body(): pl.pallas_call(finish, out_shape=[out] * 3, in_specs=[vmem] * 3, out_spec...  0.8 us

profile of v1, /device:TPU:1, one launch (start us, length us, event | category | flops | bytes accessed | tf_op | source)
XLA Modules:
  0.0 14.3 jit_solution(13497485407839287706)
XLA Ops:
  0.6 12.9 %shard_map.148 = (f32[3,9945]{1,0:T(4,128)S(1)}, f32[3,9945]{1,0:T(4,128)S(1)}, f32[3,9945]{1,0:T(4,128)S(1)}) custom-call(f32[3,1,9945]{2,1,0:T(1,128)} %bitcast.19, f32[3,1,9945]{2,1,0:T(1,128)} %bitcast.20, f32[3,1,9945]{2,1,0:T(1,128)} %bitcast.21, s32[125,1,128]{2,1,0:T(1,128)} %bitcast.22, f32[9,125,1,128]{3,2,1,0:T(1,128)} %bitcast.18, ...), custom_call_target="tpu_custom_call" | custom-call | tf_op jit(solution)/shard_map/pallas_call | solution.py:464
  13.5 0.8 %shard_map.149 = (f32[3,1,9945]{2,1,0:T(1,128)}, f32[3,1,9945]{2,1,0:T(1,128)}, f32[3,1,9945]{2,1,0:T(1,128)}) custom-call(f32[3,9945]{1,0:T(4,128)S(1)} %get-tuple-element.9.pos, f32[3,9945]{1,0:T(4,128)S(1)} %get-tuple-element.10.vel, f32[3,9945]{1,0:T(4,128)S(1)} %get-tuple-element.11.acc), custom_call_target="tpu_custom_call" | custom-call | tf_op jit(solution)/shard_map/pallas_call | solution.py:513

commit v2 on v1

v2 whole, which is shorter than its diff:
```python
import jax
import jax.numpy as jnp
import numpy as np
from jax import lax
from jax.experimental import pallas as pl
from jax.experimental.pallas import tpu as pltpu
from jax.sharding import PartitionSpec as P

EX = 4
EY = 16
EZ = 2
NX = 4 * EX + 1
NY = 4 * EY + 1
NZ = 4 * EZ + 1
PLANE = NY * NZ
CHUNKS = -(-PLANE // 128)
STRIDE = 4 * NZ
SPAN = 5 * NZ
SLOT = 48
GROWS = 56
SROW = 72
TAIL = PLANE - NZ - 128 * (CHUNKS - 1)
PITCH = 14

LIMIT = 65 * 1000 * 1000

time_step = 0.1
MESH = pl.DeviceIdType.MESH


def derivative_table():
    points = np.array([-1.0, -np.sqrt(3.0 / 7.0), 0.0, np.sqrt(3.0 / 7.0), 1.0])
    count = points.shape[0]
    weights = np.array(
        [
            1.0 / np.prod([points[s] - points[o] for o in range(count) if o != s])
            for s in range(count)
        ]
    )
    table = np.zeros((count, count))
    for t in range(count):
        for s in range(count):
            if t != s:
                table[t, s] = weights[s] / weights[t] / (points[t] - points[s])
        table[t, t] = -np.sum(table[t])
    return table


def constants():
    table = derivative_table()
    eye = np.eye(5)
    parts = [
        np.kron(table, np.kron(eye, eye)),
        np.kron(eye, np.kron(table, eye)),
        np.kron(eye, np.kron(eye, table)),
    ]
    pad = np.zeros((125, 5 * SLOT))
    for a in range(5):
        for b in range(5):
            for c in range(5):
                pad[a * 25 + 5 * b + c, a * SLOT + NZ * b + c] = 1.0
    deriv = np.zeros((384, 5 * SLOT), np.float32)
    for l in range(3):
        deriv[l * 128 : l * 128 + 125] = parts[l] @ pad
    spread = np.zeros((5 * SLOT, 128), np.float32)
    spread[:, :125] = pad.T
    return deriv, -deriv.T.copy(), spread


def split2(x):
    hi = x.astype(jnp.bfloat16)
    low = (x - hi.astype(jnp.float32)).astype(jnp.bfloat16)
    return (hi, low)


def halves(x):
    hi = np.asarray(x, jnp.bfloat16)
    low = np.asarray(x - hi.astype(np.float32), jnp.bfloat16)
    return np.stack([hi, low])


def product(pair, y):
    hi, low = split2(y)
    dot = lambda a, b: jnp.dot(a, b, preferred_element_type=jnp.float32)
    return dot(pair[0], hi) + dot(pair[0], low) + dot(pair[1], hi)


def stacked(x, y, dims):
    rows = x.shape[0]
    out = lax.dot_general(
        jnp.concatenate(split2(x), axis=0),
        y,
        (dims, ((), ())),
        preferred_element_type=jnp.float32,
    )
    return out[:rows] + out[rows:]


def ways():
    steps = (0, -1, 1)
    found = [(x, y, z) for z in steps for y in steps for x in steps][1:]
    half = [w for w in found if w > (0, 0, 0)]
    half.sort(key=lambda w: (sum(map(abs, w)), -abs(w[2])))
    other = [tuple(-v for v in w) for w in half]
    return half + other[::-1]


WAYS = ways()


def neighbours():
    names = ("gx", "gy", "gz")
    spots = [lax.axis_index(n) for n in names]
    sizes = [lax.axis_size(n) for n in names]
    links = []
    for way in WAYS:
        there = None
        peer = {}
        for n, s, z, w in zip(names, spots, sizes, way):
            if w:
                ok = s > 0 if w < 0 else s < z - 1
                there = ok if there is None else there & ok
                peer[n] = s + w
        links.append((way, there, peer))
    return links


def squeezed(ref):
    return ref.at[:, 0] if len(ref.shape) == 3 else ref.at[:, :, 0]


def kernel(
    displ, veloc, accel, node, inv, jac, lame, shear, dens,
    deriv_ref, back_ref, spread_ref,
    pos_out, vel_out, acc_out,
    deriv_s, back_s, spread_s,
    d_s, v_s, a_s, node_s, inv_s, jac_s, lame_s, shear_s, dens_s,
    nf, u_s, fl_s, md_s, grid_s,
    m_send, p_send, x_send, e_send,
    m_recv, p_recv, q_recv, x_recv, e_recv, f_recv, c_recv,
    in_sem, send_sem, recv_sem,
):
    links = neighbours()
    copies = []
    for k, (src, dst) in enumerate(((displ, d_s), (veloc, v_s), (accel, a_s))):
        for c in range(3):
            copies.append(
                pltpu.make_async_copy(
                    src.at[c], dst.at[pl.ds(c, 1)], in_sem.at[3 * k + c]
                )
            )
    elems = ((node, node_s), (inv, inv_s), (jac, jac_s), (lame, lame_s), (shear, shear_s), (dens, dens_s))
    for k, (src, dst) in enumerate(elems):
        copies.append(pltpu.make_async_copy(squeezed(src), dst, in_sem.at[9 + k]))
    consts = ((deriv_ref, deriv_s), (back_ref, back_s), (spread_ref, spread_s))
    for k, (src, dst) in enumerate(consts):
        copies.append(pltpu.make_async_copy(src, dst, in_sem.at[15 + k]))
    for cp in copies:
        cp.start()
    nf[...] = jnp.zeros_like(nf)
    u_s[...] = jnp.zeros_like(u_s)
    fl_s[...] = jnp.zeros_like(fl_s)
    md_s[...] = jnp.zeros_like(md_s)
    for ref in (m_recv, p_recv, q_recv, x_recv, e_recv, f_recv, c_recv):
        ref[...] = jnp.zeros_like(ref)
    barrier = pltpu.get_barrier_semaphore()
    for way, there, peer in links:

        @pl.when(there)
        def _():
            pl.semaphore_signal(barrier, inc=1, device_id=peer, device_id_type=MESH)

    for cp in copies[:10]:
        cp.wait()

    half = 0.5 * time_step
    pos = d_s[...] + time_step * v_s[...] + (half * time_step) * a_s[...]
    d_s[...] = pos
    vel_out[...] = v_s[...] + half * a_s[...]
    pos_out[...] = pos
    for x in range(NX):
        rows = pl.ds(x, 3, stride=16) if x < NX - 1 else pl.ds(48, 3)
        for j in range(CHUNKS):
            lanes = min(128, PLANE - 128 * j)
            at = PLANE * x + 128 * j
            nf[j, rows, 0:lanes] = d_s[:, at : at + lanes]

    corner = node_s[0:1, :].astype(jnp.float32)
    x0 = jnp.floor((corner + 0.5) * (1.0 / PLANE))
    rem = corner - PLANE * x0
    y0 = jnp.floor((rem + 0.5) * (1.0 / NZ))
    z0 = rem - NZ * y0
    upper = z0 > 1.0
    last = x0 > NX - 6.0
    iota = lax.broadcasted_iota(jnp.int32, (256, 128), 0).astype(jnp.float32)
    goal = 4.0 * y0 + x0
    picks = []
    for a in range(5):
        aim = goal + a if a < 4 else jnp.where(last, -1.0, goal + a)
        picks.append(jnp.where(iota == aim, 1.0, 0.0).astype(jnp.bfloat16))
    picks = jnp.concatenate(picks, axis=1)
    goal = 2.0 * y0
    ends = []
    for c in range(4):
        aim = jnp.where(last, goal + c, -1.0)
        ends.append(jnp.where(iota[0:128] == aim, 1.0, 0.0).astype(jnp.bfloat16))
    ends = jnp.concatenate(ends, axis=1)

    lane = lax.broadcasted_iota(jnp.int32, (1, 128), 1)
    windows = []
    for ey in range(EY):
        j, at = divmod(STRIDE * ey, 128)
        part = nf[j]
        if at + SLOT > 128:
            part = jnp.where(lane >= at, part, nf[j + 1])
        windows.append(pltpu.roll(part, 128 - at, 1) if at else part)
    turned = []
    for c in range(4):
        first, many = (16 * c, 16) if c < 3 else (48, 8)
        rows = jnp.concatenate([w[first : first + many] for w in windows], axis=0)
        turned.append(jnp.transpose(rows)[:SLOT])
    gathered = stacked(jnp.concatenate(turned[:3], axis=0), picks, ((1,), (0,)))
    beyond = stacked(turned[3], ends[:, : 3 * 128], ((1,), (0,)))
    for c in range(3):
        for a in range(5):
            part = gathered[SLOT * c : SLOT * (c + 1), 128 * a : 128 * (a + 1)]
            if a == 4:
                part = part + beyond[:, 128 * c : 128 * (c + 1)]
            part = jnp.where(upper, pltpu.roll(part, SLOT - 4, 0), part)
            u_s[SLOT * a : SLOT * (a + 1), 128 * c : 128 * (c + 1)] = part

    for cp in copies[15:]:
        cp.wait()
    local = product(deriv_s, u_s[...])
    for cp in copies[10:15]:
        cp.wait()
    grads = [
        [local[l * 128 : l * 128 + 125, c * 128 : (c + 1) * 128] for c in range(3)]
        for l in range(3)
    ]
    maps = [[inv_s[3 * l + j] for j in range(3)] for l in range(3)]
    weight = jac_s[...]
    lam = lame_s[...]
    mu = shear_s[...]
    h = [
        [sum(grads[l][c] * maps[l][j] for l in range(3)) for j in range(3)] for c in range(3)
    ]
    div = lam * (h[0][0] + h[1][1] + h[2][2])
    stress = [[None] * 3 for _ in range(3)]
    for c in range(3):
        for j in range(c, 3):
            s = mu * (h[c][j] + h[j][c])
            if c == j:
                s = s + div
            s = s * weight
            stress[c][j] = s
            stress[j][c] = s
    for l in range(3):
        for c in range(3):
            fl_s[l * 128 : l * 128 + 125, c * 128 : (c + 1) * 128] = sum(
                stress[c][j] * maps[l][j] for j in range(3)
            )
    md_s[0:125, :] = dens_s[...] * weight
    terms = product(back_s, fl_s[...])
    heavy = sum(
        jnp.dot(spread_s[...], part, preferred_element_type=jnp.float32)
        for part in split2(md_s[...])
    )

    columns = []
    tops = []
    for c in range(4):
        blocks = []
        for a in range(5):
            at = slice(SLOT * a, SLOT * (a + 1))
            part = terms[at, 128 * c : 128 * (c + 1)] if c < 3 else heavy[at]
            blocks.append(jnp.where(upper, pltpu.roll(part, 4, 0), part))
        columns.append(jnp.concatenate(blocks, axis=1))
        tops.append(blocks[4])
    placed = stacked(jnp.concatenate(columns, axis=0), picks, ((1,), (1,)))
    topped = stacked(jnp.concatenate(tops, axis=1), ends, ((1,), (1,)))
    blank = jnp.zeros((128, 128 - SLOT), jnp.float32)
    for c in range(5):
        if c < 4:
            part = placed[SLOT * c : SLOT * (c + 1)]
            halves_ = [part[:, :128], part[:, 128:]]
            first, many = 16 * c, 16
        else:
            halves_ = [topped]
            first, many = 64, 8
        back = [jnp.concatenate([jnp.transpose(h), blank], axis=1) for h in halves_]
        back = jnp.concatenate(back, axis=0) if c < 4 else back[0]
        sums = [None] * CHUNKS
        for ey in range(EY):
            j, at = divmod(STRIDE * ey, 128)
            part = back[many * ey : many * (ey + 1)]
            part = pltpu.roll(part, at, 1) if at else part
            pieces = [(j, part)]
            if at + SLOT > 128:
                pieces = [
                    (j, jnp.where(lane >= at, part, 0.0)),
                    (j + 1, jnp.where(lane < at, part, 0.0)),
                ]
            for k, piece in pieces:
                sums[k] = piece if sums[k] is None else sums[k] + piece
        for j in range(CHUNKS):
            grid_s[j, first : first + many, :] = sums[j]

    sides = (pl.ds(0, 4, stride=16), pl.ds(64, 4))
    lanes = lax.broadcasted_iota(jnp.int32, (SROW, 128), 1)
    far = CHUNKS - 1
    where_z = jnp.where(lanes < 64, NZ * lanes, NZ * (lanes - 64) + NZ - 1)
    both = None
    for j in range(CHUNKS):
        got = jnp.take_along_axis(
            grid_s[j], where_z & 127, axis=1, mode="promise_in_bounds"
        )
        both = got if both is None else jnp.where(where_z >= 128 * j, got, both)
    edge = grid_s[far]
    m_send[0] = jnp.where(lanes < 64, both, jnp.where(lanes == TAIL, edge, 0.0))
    upper_face = pltpu.roll(both, 64, 1)
    upper_edge = pltpu.roll(edge, 128 - (NZ - 1), 1)
    m_send[1] = jnp.where(lanes < 64, upper_face, jnp.where(lanes == TAIL, upper_edge, 0.0))
    rims = (grid_s[0], pltpu.roll(edge, 128 - TAIL, 1))
    lane8 = lax.broadcasted_iota(jnp.int32, (8, 128), 1)
    for side in range(2):
        for j in range(CHUNKS):
            x_send[side, j] = grid_s[j, sides[side], :]
        for dz in range(2):
            e_send[side, dz] = m_send[dz, sides[side], :]
        packed = None
        for i in range(SROW // 8):
            got = jnp.where(lane8 < NZ, rims[side][8 * i : 8 * i + 8], 0.0)
            got = pltpu.roll(got, PITCH * i, 1) if i else got
            packed = got if packed is None else packed + got
        p_send[side] = packed

    def copy(k, way, peer, arriving):
        ref_from, ref_to = route(way, arriving)
        return pltpu.make_async_remote_copy(
            src_ref=ref_from,
            dst_ref=ref_to,
            send_sem=send_sem.at[k],
            recv_sem=recv_sem.at[len(WAYS) - 1 - k if not arriving else k],
            device_id=peer,
            device_id_type=MESH,
        )

    def route(way, arriving):
        low = tuple((w + 1) // 2 for w in way)
        sx, sy, sz = low
        if arriving:
            ox, oy, oz = low
            sx, sy, sz = 1 - sx, 1 - sy, 1 - sz
        else:
            ox, oy, oz = 1 - sx, 1 - sy, 1 - sz
        dx, dy, dz = (w != 0 for w in way)
        end = far * sy
        if dx and dy and dz:
            return x_send.at[sx, end], c_recv.at[ox, oy, oz]
        if dx and dy:
            return x_send.at[sx, end], f_recv.at[ox, oy]
        if dx and dz:
            return e_send.at[sx, sz], e_recv.at[ox, oz]
        if dy and dz:
            return p_send.at[sy], q_recv.at[oy, oz]
        if dx:
            return x_send.at[sx], x_recv.at[ox]
        if dy:
            return p_send.at[sy], p_recv.at[oy]
        return m_send.at[sz], m_recv.at[oz]

    peers = sum(there.astype(jnp.int32) for way, there, peer in links)
    pl.semaphore_wait(barrier, peers)
    farthest = sorted(range(len(WAYS)), key=lambda k: -sum(map(abs, WAYS[k])))
    for k in farthest:
        way, there, peer = links[k]

        @pl.when(there)
        def _():
            copy(k, way, peer, False).start()

    for k, (way, there, peer) in enumerate(links):

        @pl.when(there)
        def _():
            copy(k, way, peer, True).wait_recv()

    for dz in range(2):
        for sx in range(2):
            m_recv[dz, sides[sx], :] += e_recv[sx, dz]
    full = [m_recv[dz] for dz in range(2)]
    strips = []
    for sy in range(2):
        sums = p_recv[sy]
        for dz in range(2):
            got = pltpu.roll(q_recv[sy, dz], 128 - 8 if dz == 0 else 8, 1)
            here = lax.rem(lane8, PITCH) == (NZ - 1) * dz
            sums = sums + jnp.where(here & (lane8 < PITCH * 9), got, 0.0)
        parts = []
        for i in range(SROW // 8):
            got = pltpu.roll(sums, 128 - PITCH * i, 1) if i else sums
            parts.append(jnp.where(lane8 < NZ, got, 0.0))
        strip = jnp.concatenate(parts, axis=0)
        strips.append(strip if sy == 0 else pltpu.roll(strip, TAIL, 1))
    lane4 = lax.broadcasted_iota(jnp.int32, (4, 128), 1)
    for sx in range(2):
        for sy in range(2):
            shift = 128 - TAIL if sy == 0 else TAIL
            first = TAIL * sy
            got = pltpu.roll(f_recv[sx, sy], shift, 1)
            got = jnp.where((lane4 >= first) & (lane4 < first + NZ), got, 0.0)
            for dz in range(2):
                turn = (shift + (128 - 8 if dz == 0 else 8)) % 128
                corner = pltpu.roll(c_recv[sx, sy, dz], turn, 1)
                got = got + jnp.where(lane4 == first + (NZ - 1) * dz, corner, 0.0)
            x_recv[sx, far * sy] += got
    for j in range(CHUNKS):
        node = lanes + 128 * j
        along = lax.div(node, NZ)
        depth = node - NZ * along
        sums = grid_s[j]
        for dz in range(2):
            got = jnp.take_along_axis(
                full[dz], jnp.minimum(along, 127), axis=1, mode="promise_in_bounds"
            )
            sums = sums + jnp.where((depth == (NZ - 1) * dz) & (along < NY), got, 0.0)
        if j == 0:
            sums = sums + strips[0]
        if j == far:
            sums = sums + strips[1]
        grid_s[j] = sums
        for sx in range(2):
            grid_s[j, sides[sx], :] += x_recv[sx, j]
        mass = grid_s[j, 48:64, :]
        for c in range(3):
            grid_s[j, 16 * c : 16 * c + 16, :] = grid_s[j, 16 * c : 16 * c + 16, :] / mass
        grid_s[j, 64:67, :] = grid_s[j, 64:67, :] / grid_s[j, 67:68, :]

    for x in range(NX):
        rows = pl.ds(x, 3, stride=16) if x < NX - 1 else pl.ds(64, 3)
        for j in range(CHUNKS):
            width = min(128, PLANE - 128 * j)
            at = PLANE * x + 128 * j
            acc_out[:, at : at + width] = grid_s[j, rows, 0:width]
    for k, (way, there, peer) in enumerate(links):

        @pl.when(there)
        def _():
            copy(k, way, peer, False).wait_send()


def finish(pos, vel, acc, pos_out, vel_out, acc_out, v_s, sem):
    def put(src, dst, k):
        copies = [
            pltpu.make_async_copy(src.at[pl.ds(c, 1)], dst.at[c], sem.at[k + c]) for c in range(3)
        ]
        for cp in copies:
            cp.start()
        return copies

    copies = put(pos, pos_out, 0) + put(acc, acc_out, 3)
    v_s[...] = vel[...] + (0.5 * time_step) * acc[...]
    for cp in copies + put(v_s, vel_out, 6):
        cp.wait()


def body(displ, veloc, accel, node_index, inv_map, jac_weight, lame_first, shear_mod, density):
    nodes = displ.shape[4]
    elements = node_index.shape[4]
    deriv, back, spread = constants()
    deriv, back = halves(deriv), halves(back)
    fields = [x.reshape(3, 1, nodes) for x in (displ, veloc, accel)]
    elems = [
        x.reshape(125, 1, elements) for x in (jac_weight, lame_first, shear_mod, density)
    ]
    vmem = pl.BlockSpec(memory_space=pltpu.VMEM)
    hbm = pl.BlockSpec(memory_space=pltpu.HBM)
    f32 = jnp.float32
    out = jax.ShapeDtypeStruct((3, 1, nodes), f32)
    elem = pltpu.VMEM((125, elements), f32)
    result = pl.pallas_call(
        kernel,
        out_shape=[pltpu.VMEM((3, nodes), f32)] * 3,
        in_specs=[hbm] * 12,
        out_specs=[vmem] * 3,
        scratch_shapes=[
            pltpu.VMEM(deriv.shape, jnp.bfloat16),
            pltpu.VMEM(back.shape, jnp.bfloat16),
            pltpu.VMEM(spread.shape, jnp.bfloat16),
            pltpu.VMEM((3, nodes), f32),
            pltpu.VMEM((3, nodes), f32),
            pltpu.VMEM((3, nodes), f32),
            pltpu.VMEM((125, elements), jnp.int32),
            pltpu.VMEM((9, 125, elements), f32),
            elem, elem, elem, elem,
            pltpu.VMEM((CHUNKS, GROWS, 128), f32),
            pltpu.VMEM((5 * SLOT, 384), f32),
            pltpu.VMEM((384, 384), f32),
            pltpu.VMEM((128, 128), f32),
            pltpu.VMEM((CHUNKS, SROW, 128), f32),
            pltpu.VMEM((2, SROW, 128), f32),
            pltpu.VMEM((2, 8, 128), f32),
            pltpu.VMEM((2, CHUNKS, 4, 128), f32),
            pltpu.VMEM((2, 2, 4, 128), f32),
            pltpu.VMEM((2, SROW, 128), f32),
            pltpu.VMEM((2, 8, 128), f32),
            pltpu.VMEM((2, 2, 8, 128), f32),
            pltpu.VMEM((2, CHUNKS, 4, 128), f32),
            pltpu.VMEM((2, 2, 4, 128), f32),
            pltpu.VMEM((2, 2, 4, 128), f32),
            pltpu.VMEM((2, 2, 2, 4, 128), f32),
            pltpu.SemaphoreType.DMA((18,)),
            pltpu.SemaphoreType.DMA((26,)),
            pltpu.SemaphoreType.DMA((26,)),
        ],
        compiler_params=pltpu.CompilerParams(
            collective_id=0, has_side_effects=True, vmem_limit_bytes=LIMIT
        ),
    )(
        *fields,
        node_index.reshape(125, 1, elements),
        inv_map.reshape(9, 125, 1, elements),
        *elems,
        jnp.asarray(deriv),
        jnp.asarray(back),
        jnp.asarray(spread, jnp.bfloat16),
    )
    final = pl.pallas_call(
        finish,
        out_shape=[out] * 3,
        in_specs=[vmem] * 3,
        out_specs=[hbm] * 3,
        scratch_shapes=[pltpu.VMEM((3, nodes), f32), pltpu.SemaphoreType.DMA((9,))],
        compiler_params=pltpu.CompilerParams(vmem_limit_bytes=LIMIT),
    )(*[pltpu.with_memory_space_constraint(x, pltpu.VMEM) for x in result])
    return tuple(x.reshape(displ.shape) for x in final)


def solution(mesh):
    field = P(None, "gx", "gy", "gz", None)
    elem = P("gx", "gy", "gz", None, None)
    placed = (field,) * 3 + (elem, P("gx", "gy", "gz", None, None, None)) + (elem,) * 4
    return jax.shard_map(
        body, mesh=mesh, in_specs=placed, out_specs=(field,) * 3, check_vma=False
    )
```

time: 14.5 us -> 13 us (0.90)
  Pallas kernels: 13.7 us -> 12.2 us
    pallas_call x1, Pallas kernels: 12.9 us -> 11.4 us  [body(): pl.pallas_call(kernel, out_shape=[pltpu.VMEM((3, nodes), f32)] * 3, in_sp...]
where the time goes in v2:
time: 13 us; the launch traced here: 12.8 us
  Pallas kernels  12.2 us (94%)
  between operations  0.64 us (5%)
    pallas_call x1, Pallas kernels, body(): pl.pallas_call(kernel, out_shape=[pltpu.VMEM((3, nodes), f32)] * 3, in_sp...  11.4 us
    pallas_call x1, Pallas kernels, body(): pl.pallas_call(finish, out_shape=[out] * 3, in_specs=[vmem] * 3, out_spec...  0.8 us

profile of v2, /device:TPU:1, one launch (start us, length us, event | category | flops | bytes accessed | tf_op | source)
XLA Modules:
  0.0 12.8 jit_solution(696070001572670804)
XLA Ops:
  0.6 11.4 %shard_map.139 = (f32[3,9945]{1,0:T(4,128)S(1)}, f32[3,9945]{1,0:T(4,128)S(1)}, f32[3,9945]{1,0:T(4,128)S(1)}) custom-call(f32[3,1,9945]{2,1,0:T(1,128)} %bitcast.19, f32[3,1,9945]{2,1,0:T(1,128)} %bitcast.20, f32[3,1,9945]{2,1,0:T(1,128)} %bitcast.21, s32[125,1,128]{2,1,0:T(1,128)} %bitcast.22, f32[9,125,1,128]{3,2,1,0:T(1,128)} %bitcast.18, ...), custom_call_target="tpu_custom_call" | custom-call | tf_op jit(solution)/shard_map/pallas_call | solution.py:482
  12.0 0.8 %shard_map.140 = (f32[3,1,9945]{2,1,0:T(1,128)}, f32[3,1,9945]{2,1,0:T(1,128)}, f32[3,1,9945]{2,1,0:T(1,128)}) custom-call(f32[3,9945]{1,0:T(4,128)S(1)} %get-tuple-element.9.pos, f32[3,9945]{1,0:T(4,128)S(1)} %get-tuple-element.10.vel, f32[3,9945]{1,0:T(4,128)S(1)} %get-tuple-element.11.acc), custom_call_target="tpu_custom_call" | custom-call | tf_op jit(solution)/shard_map/pallas_call | solution.py:529

commit v3 on v2

--- a/solution.py
+++ b/solution.py
@@ -17,7 +17,6 @@
 STRIDE = 4 * NZ
 SPAN = 5 * NZ
 SLOT = 48
-GROWS = 56
 SROW = 72
 TAIL = PLANE - NZ - 128 * (CHUNKS - 1)
 PITCH = 14
@@ -125,6 +124,23 @@
     return links
 
 
+def classes():
+    found = [((), None)]
+    for name in ("gx", "gy", "gz"):
+        size, spot = lax.axis_size(name), lax.axis_index(name)
+        inner = (spot > 0) & (spot < size - 1)
+        choices = [(min(size - 1, 1), None)]
+        if size > 2:
+            choices = [(1, jnp.logical_not(inner)), (2, inner)]
+        grown = []
+        for counts, here in found:
+            for count, ok in choices:
+                both = here if ok is None else ok if here is None else here & ok
+                grown.append((counts + (count,), both))
+        found = grown
+    return [(counts, True if here is None else here) for counts, here in found]
+
+
 def squeezed(ref):
     return ref.at[:, 0] if len(ref.shape) == 3 else ref.at[:, :, 0]
 
@@ -134,57 +150,33 @@
     deriv_ref, back_ref, spread_ref,
     pos_out, vel_out, acc_out,
     deriv_s, back_s, spread_s,
-    d_s, v_s, a_s, node_s, inv_s, jac_s, lame_s, shear_s, dens_s,
-    nf, u_s, fl_s, md_s, grid_s,
-    m_send, p_send, x_send, e_send,
+    d_s, v_s, a_s, node_s, inv_s, elem_s,
+    picks_s, ends_s, w_s, u_s, fl_s, md_s, grid_s,
+    m_send, p_send, x_send, e_send, q_send, f_send, c_send,
     m_recv, p_recv, q_recv, x_recv, e_recv, f_recv, c_recv,
-    in_sem, send_sem, recv_sem,
+    tally, in_sem, send_sem, recv_sem,
 ):
     links = neighbours()
-    copies = []
+    head = node.at[pl.ds(0, 1), 0]
+    copies = [pltpu.make_async_copy(head, node_s, in_sem.at[0])]
     for k, (src, dst) in enumerate(((displ, d_s), (veloc, v_s), (accel, a_s))):
-        for c in range(3):
-            copies.append(
-                pltpu.make_async_copy(
-                    src.at[c], dst.at[pl.ds(c, 1)], in_sem.at[3 * k + c]
-                )
-            )
-    elems = ((node, node_s), (inv, inv_s), (jac, jac_s), (lame, lame_s), (shear, shear_s), (dens, dens_s))
-    for k, (src, dst) in enumerate(elems):
-        copies.append(pltpu.make_async_copy(squeezed(src), dst, in_sem.at[9 + k]))
+        copies.append(pltpu.make_async_copy(src.at[:, 0], dst, in_sem.at[1 + k]))
+    whole = squeezed(inv)
+    copies.append(pltpu.make_async_copy(whole, inv_s, in_sem.at[4]))
+    for k, src in enumerate((jac, lame, shear, dens)):
+        copies.append(pltpu.make_async_copy(squeezed(src), elem_s.at[k], in_sem.at[5]))
     consts = ((deriv_ref, deriv_s), (back_ref, back_s), (spread_ref, spread_s))
     for k, (src, dst) in enumerate(consts):
-        copies.append(pltpu.make_async_copy(src, dst, in_sem.at[15 + k]))
+        copies.append(pltpu.make_async_copy(src, dst, in_sem.at[6 + k]))
     for cp in copies:
         cp.start()
-    nf[...] = jnp.zeros_like(nf)
+    w_s[768:, :] = jnp.zeros((128, 128), jnp.float32)
     u_s[...] = jnp.zeros_like(u_s)
     fl_s[...] = jnp.zeros_like(fl_s)
     md_s[...] = jnp.zeros_like(md_s)
     for ref in (m_recv, p_recv, q_recv, x_recv, e_recv, f_recv, c_recv):
         ref[...] = jnp.zeros_like(ref)
-    barrier = pltpu.get_barrier_semaphore()
-    for way, there, peer in links:
-
-        @pl.when(there)
-        def _():
-            pl.semaphore_signal(barrier, inc=1, device_id=peer, device_id_type=MESH)
-
-    for cp in copies[:10]:
-        cp.wait()
-
-    half = 0.5 * time_step
-    pos = d_s[...] + time_step * v_s[...] + (half * time_step) * a_s[...]
-    d_s[...] = pos
-    vel_out[...] = v_s[...] + half * a_s[...]
-    pos_out[...] = pos
-    for x in range(NX):
-        rows = pl.ds(x, 3, stride=16) if x < NX - 1 else pl.ds(48, 3)
-        for j in range(CHUNKS):
-            lanes = min(128, PLANE - 128 * j)
-            at = PLANE * x + 128 * j
-            nf[j, rows, 0:lanes] = d_s[:, at : at + lanes]
-
+    copies[0].wait()
     corner = node_s[0:1, :].astype(jnp.float32)
     x0 = jnp.floor((corner + 0.5) * (1.0 / PLANE))
     rem = corner - PLANE * x0
@@ -194,33 +186,52 @@
     last = x0 > NX - 6.0
     iota = lax.broadcasted_iota(jnp.int32, (256, 128), 0).astype(jnp.float32)
     goal = 4.0 * y0 + x0
-    picks = []
     for a in range(5):
         aim = goal + a if a < 4 else jnp.where(last, -1.0, goal + a)
-        picks.append(jnp.where(iota == aim, 1.0, 0.0).astype(jnp.bfloat16))
-    picks = jnp.concatenate(picks, axis=1)
+        picks_s[:, 128 * a : 128 * (a + 1)] = jnp.where(iota == aim, 1.0, 0.0).astype(jnp.bfloat16)
     goal = 2.0 * y0
-    ends = []
     for c in range(4):
         aim = jnp.where(last, goal + c, -1.0)
-        ends.append(jnp.where(iota[0:128] == aim, 1.0, 0.0).astype(jnp.bfloat16))
-    ends = jnp.concatenate(ends, axis=1)
+        ends_s[:, 128 * c : 128 * (c + 1)] = jnp.where(iota[0:128] == aim, 1.0, 0.0).astype(jnp.bfloat16)
+
+    barrier = pltpu.get_barrier_semaphore()
+    for way, there, peer in links:
+
+        @pl.when(there)
+        def _():
+            pl.semaphore_signal(barrier, inc=1, device_id=peer, device_id_type=MESH)
+
+    for cp in copies[1:4]:
+        cp.wait()
+
+    half = 0.5 * time_step
+    pos = d_s[...] + time_step * v_s[...] + (half * time_step) * a_s[...]
+    pos_out[...] = pos
 
     lane = lax.broadcasted_iota(jnp.int32, (1, 128), 1)
-    windows = []
-    for ey in range(EY):
-        j, at = divmod(STRIDE * ey, 128)
-        part = nf[j]
-        if at + SLOT > 128:
-            part = jnp.where(lane >= at, part, nf[j + 1])
-        windows.append(pltpu.roll(part, 128 - at, 1) if at else part)
-    turned = []
-    for c in range(4):
-        first, many = (16 * c, 16) if c < 3 else (48, 8)
-        rows = jnp.concatenate([w[first : first + many] for w in windows], axis=0)
-        turned.append(jnp.transpose(rows)[:SLOT])
-    gathered = stacked(jnp.concatenate(turned[:3], axis=0), picks, ((1,), (0,)))
-    beyond = stacked(turned[3], ends[:, : 3 * 128], ((1,), (0,)))
+
+    def chunk(q):
+        width = min(128, PLANE * NX - 128 * q)
+        part = pos_out[:, 128 * q : 128 * q + width]
+        if width < 128:
+            part = jnp.concatenate([part, jnp.zeros((3, 128 - width), jnp.float32)], axis=1)
+        return part
+
+    for x in range(NX):
+        for ey in range(EY):
+            q, at = divmod(PLANE * x + STRIDE * ey, 128)
+            part = chunk(q)
+            if at + SPAN > 128:
+                part = jnp.where(lane >= at, part, chunk(q + 1))
+            part = pltpu.roll(part, 128 - at, 1) if at else part
+            if x < NX - 1:
+                w_s[pl.ds(16 * ey + x, 3, stride=256), :] = part
+            else:
+                w_s[768 + 8 * ey : 768 + 8 * ey + 3, :] = part
+    turned = [jnp.transpose(w_s[256 * c : 256 * (c + 1), :])[:SLOT] for c in range(3)]
+    turned.append(jnp.transpose(w_s[768:896, :])[:SLOT])
+    gathered = stacked(jnp.concatenate(turned[:3], axis=0), picks_s[...], ((1,), (0,)))
+    beyond = stacked(turned[3], ends_s[:, : 3 * 128], ((1,), (0,)))
     for c in range(3):
         for a in range(5):
             part = gathered[SLOT * c : SLOT * (c + 1), 128 * a : 128 * (a + 1)]
@@ -229,19 +240,17 @@
             part = jnp.where(upper, pltpu.roll(part, SLOT - 4, 0), part)
             u_s[SLOT * a : SLOT * (a + 1), 128 * c : 128 * (c + 1)] = part
 
-    for cp in copies[15:]:
+    for cp in copies[9:]:
         cp.wait()
     local = product(deriv_s, u_s[...])
-    for cp in copies[10:15]:
-        cp.wait()
+    copies[4].wait()
+    pltpu.make_async_copy(whole.at[pl.ds(0, 4)], elem_s, in_sem.at[5]).wait()
     grads = [
         [local[l * 128 : l * 128 + 125, c * 128 : (c + 1) * 128] for c in range(3)]
         for l in range(3)
     ]
     maps = [[inv_s[3 * l + j] for j in range(3)] for l in range(3)]
-    weight = jac_s[...]
-    lam = lame_s[...]
-    mu = shear_s[...]
+    weight, lam, mu, dens_e = (elem_s[k] for k in range(4))
     h = [
         [sum(grads[l][c] * maps[l][j] for l in range(3)) for j in range(3)] for c in range(3)
     ]
@@ -260,7 +269,7 @@
             fl_s[l * 128 : l * 128 + 125, c * 128 : (c + 1) * 128] = sum(
                 stress[c][j] * maps[l][j] for j in range(3)
             )
-    md_s[0:125, :] = dens_s[...] * weight
+    md_s[0:125, :] = dens_e * weight
     terms = product(back_s, fl_s[...])
     heavy = sum(
         jnp.dot(spread_s[...], part, preferred_element_type=jnp.float32)
@@ -277,8 +286,8 @@
             blocks.append(jnp.where(upper, pltpu.roll(part, 4, 0), part))
         columns.append(jnp.concatenate(blocks, axis=1))
         tops.append(blocks[4])
-    placed = stacked(jnp.concatenate(columns, axis=0), picks, ((1,), (1,)))
-    topped = stacked(jnp.concatenate(tops, axis=1), ends, ((1,), (1,)))
+    placed = stacked(jnp.concatenate(columns, axis=0), picks_s[...], ((1,), (1,)))
+    topped = stacked(jnp.concatenate(tops, axis=1), ends_s[...], ((1,), (1,)))
     blank = jnp.zeros((128, 128 - SLOT), jnp.float32)
     for c in range(5):
         if c < 4:
@@ -309,82 +318,103 @@
     sides = (pl.ds(0, 4, stride=16), pl.ds(64, 4))
     lanes = lax.broadcasted_iota(jnp.int32, (SROW, 128), 1)
     far = CHUNKS - 1
-    where_z = jnp.where(lanes < 64, NZ * lanes, NZ * (lanes - 64) + NZ - 1)
-    both = None
-    for j in range(CHUNKS):
-        got = jnp.take_along_axis(
-            grid_s[j], where_z & 127, axis=1, mode="promise_in_bounds"
-        )
-        both = got if both is None else jnp.where(where_z >= 128 * j, got, both)
     edge = grid_s[far]
-    m_send[0] = jnp.where(lanes < 64, both, jnp.where(lanes == TAIL, edge, 0.0))
-    upper_face = pltpu.roll(both, 64, 1)
-    upper_edge = pltpu.roll(edge, 128 - (NZ - 1), 1)
-    m_send[1] = jnp.where(lanes < 64, upper_face, jnp.where(lanes == TAIL, upper_edge, 0.0))
     rims = (grid_s[0], pltpu.roll(edge, 128 - TAIL, 1))
     lane8 = lax.broadcasted_iota(jnp.int32, (8, 128), 1)
     for side in range(2):
         for j in range(CHUNKS):
             x_send[side, j] = grid_s[j, sides[side], :]
-        for dz in range(2):
-            e_send[side, dz] = m_send[dz, sides[side], :]
+    for sy in range(2):
+        rows = jnp.concatenate([x_send[0, far * sy], x_send[1, far * sy]], axis=0)
+        shift, first = (TAIL, TAIL) if sy == 0 else (128 - TAIL, 0)
+        got = pltpu.roll(rows, shift, 1)
+        got = jnp.where((lane8 >= first) & (lane8 < first + NZ), got, 0.0)
+        f_send[0, sy] = got[:4]
+        f_send[1, sy] = got[4:]
+        for sz in range(2):
+            got = pltpu.roll(rows, (shift + (8 if sz == 0 else 128 - 8)) % 128, 1)
+            got = jnp.where(lane8 == first + (NZ - 1) * (1 - sz), got, 0.0)
+            c_send[0, sy, sz] = got[:4]
+            c_send[1, sy, sz] = got[4:]
         packed = None
         for i in range(SROW // 8):
-            got = jnp.where(lane8 < NZ, rims[side][8 * i : 8 * i + 8], 0.0)
+            got = jnp.where(lane8 < NZ, rims[sy][8 * i : 8 * i + 8], 0.0)
             got = pltpu.roll(got, PITCH * i, 1) if i else got
             packed = got if packed is None else packed + got
-        p_send[side] = packed
-
-    def copy(k, way, peer, arriving):
-        ref_from, ref_to = route(way, arriving)
-        return pltpu.make_async_remote_copy(
-            src_ref=ref_from,
-            dst_ref=ref_to,
-            send_sem=send_sem.at[k],
-            recv_sem=recv_sem.at[len(WAYS) - 1 - k if not arriving else k],
-            device_id=peer,
-            device_id_type=MESH,
-        )
-
-    def route(way, arriving):
-        low = tuple((w + 1) // 2 for w in way)
-        sx, sy, sz = low
-        if arriving:
-            ox, oy, oz = low
-            sx, sy, sz = 1 - sx, 1 - sy, 1 - sz
-        else:
-            ox, oy, oz = 1 - sx, 1 - sy, 1 - sz
+        p_send[sy] = packed
+        place = lax.rem(lane8, PITCH)
+        for sz in range(2):
+            got = jnp.where(place == (NZ - 1) * sz, packed, 0.0)
+            q_send[sy, sz] = pltpu.roll(got, 8 if sz == 0 else 128 - 8, 1)
+
+    def route(way):
+        sx, sy, sz = ((w + 1) // 2 for w in way)
+        ox, oy, oz = 1 - sx, 1 - sy, 1 - sz
         dx, dy, dz = (w != 0 for w in way)
-        end = far * sy
         if dx and dy and dz:
-            return x_send.at[sx, end], c_recv.at[ox, oy, oz]
+            return c_send.at[sx, sy, sz], c_recv.at[ox, oy, oz]
         if dx and dy:
-            return x_send.at[sx, end], f_recv.at[ox, oy]
+            return f_send.at[sx, sy], f_recv.at[ox, oy]
         if dx and dz:
             return e_send.at[sx, sz], e_recv.at[ox, oz]
         if dy and dz:
-            return p_send.at[sy], q_recv.at[oy, oz]
+            return q_send.at[sy, sz], q_recv.at[oy, oz]
         if dx:
             return x_send.at[sx], x_recv.at[ox]
         if dy:
             return p_send.at[sy], p_recv.at[oy]
         return m_send.at[sz], m_recv.at[oz]
 
+    def copy(source, target, peer):
+        return pltpu.make_async_remote_copy(
+            src_ref=source,
+            dst_ref=target,
+            send_sem=send_sem.at[0],
+            recv_sem=recv_sem.at[0],
+            device_id=peer,
+            device_id_type=MESH,
+        )
+
+    def await_all(settle):
+        for (nx, ny, nz), here in classes():
+            count = nx * CHUNKS + nx * ny + nx * nz + nx * ny * nz
+            count += 2 * ny + 2 * ny * nz + nz * SROW // 4
+            whole = tally.at[pl.ds(0, count)]
+
+            @pl.when(here)
+            def _():
+                settle(copy(whole, whole, links[0][2]))
+
     peers = sum(there.astype(jnp.int32) for way, there, peer in links)
     pl.semaphore_wait(barrier, peers)
     farthest = sorted(range(len(WAYS)), key=lambda k: -sum(map(abs, WAYS[k])))
-    for k in farthest:
-        way, there, peer = links[k]
-
-        @pl.when(there)
-        def _():
-            copy(k, way, peer, False).start()
-
-    for k, (way, there, peer) in enumerate(links):
-
-        @pl.when(there)
-        def _():
-            copy(k, way, peer, True).wait_recv()
+
+    def depart(chosen):
+        for k in farthest:
+            way, there, peer = links[k]
+            if chosen(way):
+
+                @pl.when(there)
+                def _():
+                    copy(*route(way), peer).start()
+
+    flat = lambda way: way[1] == 0 and way[2] != 0
+    depart(lambda way: not flat(way))
+    for dz in range(2):
+        face = None
+        source = jnp.minimum(NZ * lanes + (NZ - 1) * dz, 128 * CHUNKS - 1)
+        for j in range(CHUNKS):
+            got = jnp.take_along_axis(
+                grid_s[j], source & 127, axis=1, mode="promise_in_bounds"
+            )
+            face = got if face is None else jnp.where(source >= 128 * j, got, face)
+        m_send[dz] = jnp.where(lanes < NY, face, 0.0)
+        for side in range(2):
+            e_send[side, dz] = m_send[dz, sides[side], :]
+    depart(flat)
+    vel_out[...] = v_s[...] + half * a_s[...]
+
+    await_all(lambda copied: copied.wait_recv())
 
     for dz in range(2):
         for sx in range(2):
@@ -392,29 +422,17 @@
     full = [m_recv[dz] for dz in range(2)]
     strips = []
     for sy in range(2):
-        sums = p_recv[sy]
-        for dz in range(2):
-            got = pltpu.roll(q_recv[sy, dz], 128 - 8 if dz == 0 else 8, 1)
-            here = lax.rem(lane8, PITCH) == (NZ - 1) * dz
-            sums = sums + jnp.where(here & (lane8 < PITCH * 9), got, 0.0)
+        sums = p_recv[sy] + q_recv[sy, 0] + q_recv[sy, 1]
         parts = []
         for i in range(SROW // 8):
-            got = pltpu.roll(sums, 128 - PITCH * i, 1) if i else sums
-            parts.append(jnp.where(lane8 < NZ, got, 0.0))
-        strip = jnp.concatenate(parts, axis=0)
-        strips.append(strip if sy == 0 else pltpu.roll(strip, TAIL, 1))
-    lane4 = lax.broadcasted_iota(jnp.int32, (4, 128), 1)
-    for sx in range(2):
-        for sy in range(2):
-            shift = 128 - TAIL if sy == 0 else TAIL
-            first = TAIL * sy
-            got = pltpu.roll(f_recv[sx, sy], shift, 1)
-            got = jnp.where((lane4 >= first) & (lane4 < first + NZ), got, 0.0)
-            for dz in range(2):
-                turn = (shift + (128 - 8 if dz == 0 else 8)) % 128
-                corner = pltpu.roll(c_recv[sx, sy, dz], turn, 1)
-                got = got + jnp.where(lane4 == first + (NZ - 1) * dz, corner, 0.0)
-            x_recv[sx, far * sy] += got
+            shift = (TAIL * sy - PITCH * i) % 128
+            got = pltpu.roll(sums, shift, 1) if shift else sums
+            parts.append(
+                jnp.where((lane8 >= TAIL * sy) & (lane8 < TAIL * sy + NZ), got, 0.0)
+            )
+        strips.append(jnp.concatenate(parts, axis=0))
+        for sx in range(2):
+            x_recv[sx, far * sy] += f_recv[sx, sy] + (c_recv[sx, sy, 0] + c_recv[sx, sy, 1])
     for j in range(CHUNKS):
         node = lanes + 128 * j
         along = lax.div(node, NZ)
@@ -443,25 +461,19 @@
             width = min(128, PLANE - 128 * j)
             at = PLANE * x + 128 * j
             acc_out[:, at : at + width] = grid_s[j, rows, 0:width]
-    for k, (way, there, peer) in enumerate(links):
-
-        @pl.when(there)
-        def _():
-            copy(k, way, peer, False).wait_send()
+    await_all(lambda copied: copied.wait_send())
 
 
 def finish(pos, vel, acc, pos_out, vel_out, acc_out, v_s, sem):
     def put(src, dst, k):
-        copies = [
-            pltpu.make_async_copy(src.at[pl.ds(c, 1)], dst.at[c], sem.at[k + c]) for c in range(3)
-        ]
-        for cp in copies:
-            cp.start()
-        return copies
-
-    copies = put(pos, pos_out, 0) + put(acc, acc_out, 3)
+        copy = pltpu.make_async_copy(src, dst.at[:, 0], sem.at[k])
+        copy.start()
+        return copy
+
+    copies = [put(pos, pos_out, 0), put(acc, acc_out, 1)]
     v_s[...] = vel[...] + (0.5 * time_step) * acc[...]
-    for cp in copies + put(v_s, vel_out, 6):
+    copies.append(put(v_s, vel_out, 2))
+    for cp in copies:
         cp.wait()
 
 
@@ -478,7 +490,6 @@
     hbm = pl.BlockSpec(memory_space=pltpu.HBM)
     f32 = jnp.float32
     out = jax.ShapeDtypeStruct((3, 1, nodes), f32)
-    elem = pltpu.VMEM((125, elements), f32)
     result = pl.pallas_call(
         kernel,
         out_shape=[pltpu.VMEM((3, nodes), f32)] * 3,
@@ -491,10 +502,12 @@
             pltpu.VMEM((3, nodes), f32),
             pltpu.VMEM((3, nodes), f32),
             pltpu.VMEM((3, nodes), f32),
-            pltpu.VMEM((125, elements), jnp.int32),
+            pltpu.VMEM((1, elements), jnp.int32),
             pltpu.VMEM((9, 125, elements), f32),
-            elem, elem, elem, elem,
-            pltpu.VMEM((CHUNKS, GROWS, 128), f32),
+            pltpu.VMEM((4, 125, elements), f32),
+            pltpu.VMEM((256, 5 * 128), jnp.bfloat16),
+            pltpu.VMEM((128, 4 * 128), jnp.bfloat16),
+            pltpu.VMEM((896, 128), f32),
             pltpu.VMEM((5 * SLOT, 384), f32),
             pltpu.VMEM((384, 384), f32),
             pltpu.VMEM((128, 128), f32),
@@ -503,6 +516,9 @@
             pltpu.VMEM((2, 8, 128), f32),
             pltpu.VMEM((2, CHUNKS, 4, 128), f32),
             pltpu.VMEM((2, 2, 4, 128), f32),
+            pltpu.VMEM((2, 2, 8, 128), f32),
+            pltpu.VMEM((2, 2, 4, 128), f32),
+            pltpu.VMEM((2, 2, 2, 4, 128), f32),
             pltpu.VMEM((2, SROW, 128), f32),
             pltpu.VMEM((2, 8, 128), f32),
             pltpu.VMEM((2, 2, 8, 128), f32),
@@ -510,9 +526,10 @@
             pltpu.VMEM((2, 2, 4, 128), f32),
             pltpu.VMEM((2, 2, 4, 128), f32),
             pltpu.VMEM((2, 2, 2, 4, 128), f32),
-            pltpu.SemaphoreType.DMA((18,)),
-            pltpu.SemaphoreType.DMA((26,)),
-            pltpu.SemaphoreType.DMA((26,)),
+            pltpu.VMEM((2 * SROW // 4 + 2 * CHUNKS + 28, 4, 128), f32),
+            pltpu.SemaphoreType.DMA((9,)),
+            pltpu.SemaphoreType.DMA((1,)),
+            pltpu.SemaphoreType.DMA((1,)),
         ],
         compiler_params=pltpu.CompilerParams(
             collective_id=0, has_side_effects=True, vmem_limit_bytes=LIMIT
@@ -531,7 +548,7 @@
         out_shape=[out] * 3,
         in_specs=[vmem] * 3,
         out_specs=[hbm] * 3,
-        scratch_shapes=[pltpu.VMEM((3, nodes), f32), pltpu.SemaphoreType.DMA((9,))],
+        scratch_shapes=[pltpu.VMEM((3, nodes), f32), pltpu.SemaphoreType.DMA((3,))],
         compiler_params=pltpu.CompilerParams(vmem_limit_bytes=LIMIT),
     )(*[pltpu.with_memory_space_constraint(x, pltpu.VMEM) for x in result])
     return tuple(x.reshape(displ.shape) for x in final)

time: 13 us -> 12.1 us (0.931)
  Pallas kernels: 12.2 us -> 11.3 us
    pallas_call x1, Pallas kernels: 11.4 us -> 10.6 us  [body(): pl.pallas_call(kernel, out_shape=[pltpu.VMEM((3, nodes), f32)] * 3, in_sp...]
where the time goes in v3:
time: 12.1 us; the launch traced here: 12 us
  Pallas kernels  11.3 us (93%)
  between operations  0.64 us (5%)
    pallas_call x1, Pallas kernels, body(): pl.pallas_call(kernel, out_shape=[pltpu.VMEM((3, nodes), f32)] * 3, in_sp...  10.6 us
    pallas_call x1, Pallas kernels, body(): pl.pallas_call(finish, out_shape=[out] * 3, in_specs=[vmem] * 3, out_spec...  0.76 us

profile of v3, /device:TPU:1, one launch (start us, length us, event | category | flops | bytes accessed | tf_op | source)
XLA Modules:
  0.0 12.0 jit_solution(1789624097791913998)
XLA Ops:
  0.6 10.6 %shard_map.139 = (f32[3,9945]{1,0:T(4,128)S(1)}, f32[3,9945]{1,0:T(4,128)S(1)}, f32[3,9945]{1,0:T(4,128)S(1)}) custom-call(f32[3,1,9945]{2,1,0:T(1,128)} %bitcast.19, f32[3,1,9945]{2,1,0:T(1,128)} %bitcast.20, f32[3,1,9945]{2,1,0:T(1,128)} %bitcast.21, s32[125,1,128]{2,1,0:T(1,128)} %bitcast.22, f32[9,125,1,128]{3,2,1,0:T(1,128)} %bitcast.18, ...), custom_call_target="tpu_custom_call" | custom-call | tf_op jit(solution)/shard_map/pallas_call | solution.py:493
  11.2 0.8 %shard_map.140 = (f32[3,1,9945]{2,1,0:T(1,128)}, f32[3,1,9945]{2,1,0:T(1,128)}, f32[3,1,9945]{2,1,0:T(1,128)}) custom-call(f32[3,9945]{1,0:T(4,128)S(1)} %get-tuple-element.9.pos, f32[3,9945]{1,0:T(4,128)S(1)} %get-tuple-element.10.vel, f32[3,9945]{1,0:T(4,128)S(1)} %get-tuple-element.11.acc), custom_call_target="tpu_custom_call" | custom-call | tf_op jit(solution)/shard_map/pallas_call | solution.py:546

commit v4 on v3

--- a/solution.py
+++ b/solution.py
@@ -20,6 +20,8 @@
 SROW = 72
 TAIL = PLANE - NZ - 128 * (CHUNKS - 1)
 PITCH = 14
+SPLITS = ((0, 7), (7, 6))
+PAIRS = tuple(((c, a), (c, a + 1)) for c in range(4) for a in (0, 2))
 
 LIMIT = 65 * 1000 * 1000
 
@@ -84,17 +86,6 @@
     return dot(pair[0], hi) + dot(pair[0], low) + dot(pair[1], hi)
 
 
-def stacked(x, y, dims):
-    rows = x.shape[0]
-    out = lax.dot_general(
-        jnp.concatenate(split2(x), axis=0),
-        y,
-        (dims, ((), ())),
-        preferred_element_type=jnp.float32,
-    )
-    return out[:rows] + out[rows:]
-
-
 def ways():
     steps = (0, -1, 1)
     found = [(x, y, z) for z in steps for y in steps for x in steps][1:]
@@ -150,8 +141,8 @@
     deriv_ref, back_ref, spread_ref,
     pos_out, vel_out, acc_out,
     deriv_s, back_s, spread_s,
-    d_s, v_s, a_s, node_s, inv_s, elem_s,
-    picks_s, ends_s, w_s, u_s, fl_s, md_s, grid_s,
+    d_s, v_s, a_s, node_s, raw_s,
+    order_s, sorted_s, w_s, z_s, top_s, u_s, fl_s, md_s, grid_s,
     m_send, p_send, x_send, e_send, q_send, f_send, c_send,
     m_recv, p_recv, q_recv, x_recv, e_recv, f_recv, c_recv,
     tally, in_sem, send_sem, recv_sem,
@@ -162,15 +153,16 @@
     for k, (src, dst) in enumerate(((displ, d_s), (veloc, v_s), (accel, a_s))):
         copies.append(pltpu.make_async_copy(src.at[:, 0], dst, in_sem.at[1 + k]))
     whole = squeezed(inv)
-    copies.append(pltpu.make_async_copy(whole, inv_s, in_sem.at[4]))
+    point = pl.ds(0, 125)
+    copies.append(pltpu.make_async_copy(whole, raw_s.at[pl.ds(0, 9), point], in_sem.at[4]))
     for k, src in enumerate((jac, lame, shear, dens)):
-        copies.append(pltpu.make_async_copy(squeezed(src), elem_s.at[k], in_sem.at[5]))
+        copies.append(pltpu.make_async_copy(squeezed(src), raw_s.at[9 + k, point], in_sem.at[5]))
     consts = ((deriv_ref, deriv_s), (back_ref, back_s), (spread_ref, spread_s))
     for k, (src, dst) in enumerate(consts):
         copies.append(pltpu.make_async_copy(src, dst, in_sem.at[6 + k]))
     for cp in copies:
         cp.start()
-    w_s[768:, :] = jnp.zeros((128, 128), jnp.float32)
+    z_s[...] = jnp.zeros_like(z_s)
     u_s[...] = jnp.zeros_like(u_s)
     fl_s[...] = jnp.zeros_like(fl_s)
     md_s[...] = jnp.zeros_like(md_s)
@@ -182,18 +174,12 @@
     rem = corner - PLANE * x0
     y0 = jnp.floor((rem + 0.5) * (1.0 / NZ))
     z0 = rem - NZ * y0
-    upper = z0 > 1.0
-    last = x0 > NX - 6.0
-    iota = lax.broadcasted_iota(jnp.int32, (256, 128), 0).astype(jnp.float32)
-    goal = 4.0 * y0 + x0
-    for a in range(5):
-        aim = goal + a if a < 4 else jnp.where(last, -1.0, goal + a)
-        picks_s[:, 128 * a : 128 * (a + 1)] = jnp.where(iota == aim, 1.0, 0.0).astype(jnp.bfloat16)
-    goal = 2.0 * y0
-    for c in range(4):
-        aim = jnp.where(last, goal + c, -1.0)
-        ends_s[:, 128 * c : 128 * (c + 1)] = jnp.where(iota[0:128] == aim, 1.0, 0.0).astype(jnp.bfloat16)
-
+    goal = EY * EX * 0.25 * z0 + EX * 0.25 * y0 + 0.25 * x0
+    goal = jnp.transpose(jnp.broadcast_to(goal, (128, 128)))
+    slots = lax.broadcasted_iota(jnp.int32, (128, 128), 1).astype(jnp.float32)
+    order = jnp.where(slots == goal, 1.0, 0.0).astype(jnp.bfloat16)
+    order_s[0:128, :] = order
+    order_s[128:256, :] = order
     barrier = pltpu.get_barrier_semaphore()
     for way, there, peer in links:
 
@@ -217,40 +203,79 @@
             part = jnp.concatenate([part, jnp.zeros((3, 128 - width), jnp.float32)], axis=1)
         return part
 
+    ahead = (4 * PLANE - STRIDE) // 128
+    blank = jnp.zeros((3, 128), jnp.float32)
+    single = [chunk(q) for q in range(-(-PLANE * NX // 128))]
+    double = [
+        jnp.concatenate([v, single[q + ahead] if q + ahead < len(single) else blank], axis=0)
+        for q, v in enumerate(single)
+    ]
+
+    def window(source, x, ey):
+        q, at = divmod(PLANE * x + STRIDE * ey, 128)
+        part = source[q]
+        if at + SPAN > 128:
+            part = jnp.where(lane >= at, part, source[q + 1])
+        return pltpu.roll(part, 128 - at, 1) if at else part
+
+    def keep(x, ey, part):
+        ex, a = divmod(x, 4)
+        spots = [(a, ex)] if x < NX - 1 else []
+        if x and a == 0:
+            spots.append((4, ex - 1))
+        for a, ex in spots:
+            first = 3 * ((a * EY + ey) * EX + ex)
+            w_s[first : first + 3, :] = part
+
     for x in range(NX):
+        paired = x < NX - 1 and x % 8 < 4
         for ey in range(EY):
-            q, at = divmod(PLANE * x + STRIDE * ey, 128)
-            part = chunk(q)
-            if at + SPAN > 128:
-                part = jnp.where(lane >= at, part, chunk(q + 1))
-            part = pltpu.roll(part, 128 - at, 1) if at else part
-            if x < NX - 1:
-                w_s[pl.ds(16 * ey + x, 3, stride=256), :] = part
-            else:
-                w_s[768 + 8 * ey : 768 + 8 * ey + 3, :] = part
-    turned = [jnp.transpose(w_s[256 * c : 256 * (c + 1), :])[:SLOT] for c in range(3)]
-    turned.append(jnp.transpose(w_s[768:896, :])[:SLOT])
-    gathered = stacked(jnp.concatenate(turned[:3], axis=0), picks_s[...], ((1,), (0,)))
-    beyond = stacked(turned[3], ends_s[:, : 3 * 128], ((1,), (0,)))
-    for c in range(3):
-        for a in range(5):
-            part = gathered[SLOT * c : SLOT * (c + 1), 128 * a : 128 * (a + 1)]
-            if a == 4:
-                part = part + beyond[:, 128 * c : 128 * (c + 1)]
-            part = jnp.where(upper, pltpu.roll(part, SLOT - 4, 0), part)
-            u_s[SLOT * a : SLOT * (a + 1), 128 * c : 128 * (c + 1)] = part
-
-    for cp in copies[9:]:
-        cp.wait()
+            if paired:
+                part = window(double, x, ey)
+                keep(x, ey, part[:3])
+                if ey:
+                    keep(x + 4, ey - 1, part[3:])
+            elif x == NX - 1 or ey == EY - 1:
+                keep(x, ey, window(single, x, ey))
+
+    copies[4].wait()
+    pltpu.make_async_copy(
+        whole.at[pl.ds(0, 4)], raw_s.at[pl.ds(9, 4), point], in_sem.at[5]
+    ).wait()
+    copies[9].wait()
+    for first, many in SPLITS:
+        raw = raw_s[first : first + many].reshape(many * 128, 128)
+        sorted_s[first : first + many] = jnp.dot(
+            jnp.concatenate(split2(raw), axis=1),
+            order_s[...],
+            preferred_element_type=jnp.float32,
+        ).reshape(many, 128, 128)
+
+    left = lax.broadcasted_iota(jnp.int32, (SLOT, 128), 1) < 64
+    each = EX * EY
+
+    def block(c, a):
+        return w_s[pl.ds(3 * each * a + c, each, stride=3), :]
+
+    for (c, a), (d, b) in PAIRS[:6] + (((0, 4), (1, 4)), ((2, 4), (2, 4))):
+        turned = jnp.transpose(jnp.concatenate([block(c, a), block(d, b)], axis=0))[:SLOT]
+        other = pltpu.roll(turned, 64, 1)
+        rise = lambda v: pltpu.roll(v, SLOT - 4, 0)
+        u_s[SLOT * a : SLOT * (a + 1), 128 * c : 128 * (c + 1)] = jnp.where(
+            left, turned, rise(other)
+        )
+        if (c, a) != (d, b):
+            u_s[SLOT * b : SLOT * (b + 1), 128 * d : 128 * (d + 1)] = jnp.where(
+                left, other, rise(turned)
+            )
+
     local = product(deriv_s, u_s[...])
-    copies[4].wait()
-    pltpu.make_async_copy(whole.at[pl.ds(0, 4)], elem_s, in_sem.at[5]).wait()
     grads = [
         [local[l * 128 : l * 128 + 125, c * 128 : (c + 1) * 128] for c in range(3)]
         for l in range(3)
     ]
-    maps = [[inv_s[3 * l + j] for j in range(3)] for l in range(3)]
-    weight, lam, mu, dens_e = (elem_s[k] for k in range(4))
+    maps = [[sorted_s[3 * l + j, 0:125] for j in range(3)] for l in range(3)]
+    weight, lam, mu, dens_e = (sorted_s[9 + k, 0:125] for k in range(4))
     h = [
         [sum(grads[l][c] * maps[l][j] for l in range(3)) for j in range(3)] for c in range(3)
     ]
@@ -270,39 +295,46 @@
                 stress[c][j] * maps[l][j] for j in range(3)
             )
     md_s[0:125, :] = dens_e * weight
+    for cp in copies[10:]:
+        cp.wait()
     terms = product(back_s, fl_s[...])
     heavy = sum(
         jnp.dot(spread_s[...], part, preferred_element_type=jnp.float32)
         for part in split2(md_s[...])
     )
 
-    columns = []
-    tops = []
-    for c in range(4):
-        blocks = []
-        for a in range(5):
-            at = slice(SLOT * a, SLOT * (a + 1))
-            part = terms[at, 128 * c : 128 * (c + 1)] if c < 3 else heavy[at]
-            blocks.append(jnp.where(upper, pltpu.roll(part, 4, 0), part))
-        columns.append(jnp.concatenate(blocks, axis=1))
-        tops.append(blocks[4])
-    placed = stacked(jnp.concatenate(columns, axis=0), picks_s[...], ((1,), (1,)))
-    topped = stacked(jnp.concatenate(tops, axis=1), ends_s[...], ((1,), (1,)))
-    blank = jnp.zeros((128, 128 - SLOT), jnp.float32)
+    def term(c, a):
+        at = slice(SLOT * a, SLOT * (a + 1))
+        return terms[at, 128 * c : 128 * (c + 1)] if c < 3 else heavy[at]
+
+    sink = lambda v: pltpu.roll(v, 4, 0)
+    tail = jnp.zeros((128, 128 - SLOT), jnp.float32)
+    crest = {}
+    rows = lax.broadcasted_iota(jnp.int32, (each, 128), 0)
+    for (c, a), (d, b) in (((0, 4), (1, 4)), ((2, 4), (3, 4))) + PAIRS:
+        one, two = term(c, a), term(d, b)
+        both = jnp.where(left, one, sink(two)) + pltpu.roll(jnp.where(left, two, sink(one)), 64, 1)
+        turned = jnp.concatenate([jnp.transpose(both), tail], axis=1)
+        for k, part in (((c, a), turned[:each]), ((d, b), turned[each:])):
+            if k[1] == 4:
+                top_s[each * k[0] : each * (k[0] + 1), :] = part
+                crest[k[0]] = jnp.where(rows % EX == 0, 0.0, pltpu.roll(part, 1, 0))
+                continue
+            if k[1] == 0:
+                part = part + crest[k[0]]
+            for ey in range(EY):
+                first = ((k[0] * EY + ey) * 4 + k[1]) * EX
+                z_s[first : first + EX, :] = part[EX * ey : EX * (ey + 1)]
     for c in range(5):
-        if c < 4:
-            part = placed[SLOT * c : SLOT * (c + 1)]
-            halves_ = [part[:, :128], part[:, 128:]]
-            first, many = 16 * c, 16
-        else:
-            halves_ = [topped]
-            first, many = 64, 8
-        back = [jnp.concatenate([jnp.transpose(h), blank], axis=1) for h in halves_]
-        back = jnp.concatenate(back, axis=0) if c < 4 else back[0]
+        first, many = (16 * c, 16) if c < 4 else (64, 8)
         sums = [None] * CHUNKS
         for ey in range(EY):
             j, at = divmod(STRIDE * ey, 128)
-            part = back[many * ey : many * (ey + 1)]
+            if c < 4:
+                part = z_s[16 * (c * EY + ey) : 16 * (c * EY + ey + 1), :]
+            else:
+                part = top_s[pl.ds(EX * ey + EX - 1, 4, stride=each), :]
+                part = jnp.concatenate([part, jnp.zeros((4, 128), jnp.float32)], axis=0)
             part = pltpu.roll(part, at, 1) if at else part
             pieces = [(j, part)]
             if at + SLOT > 128:
@@ -456,7 +488,7 @@
         grid_s[j, 64:67, :] = grid_s[j, 64:67, :] / grid_s[j, 67:68, :]
 
     for x in range(NX):
-        rows = pl.ds(x, 3, stride=16) if x < NX - 1 else pl.ds(64, 3)
+        rows = pl.ds(4 * (x % 4) + x // 4, 3, stride=16) if x < NX - 1 else pl.ds(64, 3)
         for j in range(CHUNKS):
             width = min(128, PLANE - 128 * j)
             at = PLANE * x + 128 * j
@@ -503,11 +535,12 @@
             pltpu.VMEM((3, nodes), f32),
             pltpu.VMEM((3, nodes), f32),
             pltpu.VMEM((1, elements), jnp.int32),
-            pltpu.VMEM((9, 125, elements), f32),
-            pltpu.VMEM((4, 125, elements), f32),
-            pltpu.VMEM((256, 5 * 128), jnp.bfloat16),
-            pltpu.VMEM((128, 4 * 128), jnp.bfloat16),
-            pltpu.VMEM((896, 128), f32),
+            pltpu.VMEM((13, 128, elements), f32),
+            pltpu.VMEM((256, 128), jnp.bfloat16),
+            pltpu.VMEM((13, 128, 128), f32),
+            pltpu.VMEM((15 * EX * EY, 128), f32),
+            pltpu.VMEM((16 * EX * EY, 128), f32),
+            pltpu.VMEM((4 * EX * EY, 128), f32),
             pltpu.VMEM((5 * SLOT, 384), f32),
             pltpu.VMEM((384, 384), f32),
             pltpu.VMEM((128, 128), f32),

time: 12.1 us -> 11.6 us (0.959)
  Pallas kernels: 11.3 us -> 10.8 us
    pallas_call x1, Pallas kernels: 10.6 us -> 10.1 us  [body(): pl.pallas_call(kernel, out_shape=[pltpu.VMEM((3, nodes), f32)] * 3, in_sp...]
where the time goes in v4:
time: 11.6 us; the launch traced here: 11.5 us
  Pallas kernels  10.8 us (93%)
  between operations  0.64 us (6%)
    pallas_call x1, Pallas kernels, body(): pl.pallas_call(kernel, out_shape=[pltpu.VMEM((3, nodes), f32)] * 3, in_sp...  10.1 us
    pallas_call x1, Pallas kernels, body(): pl.pallas_call(finish, out_shape=[out] * 3, in_specs=[vmem] * 3, out_spec...  0.76 us

profile of v4, /device:TPU:1, one launch (start us, length us, event | category | flops | bytes accessed | tf_op | source)
XLA Modules:
  0.0 11.5 jit_solution(3048805699220094909)
XLA Ops:
  0.6 10.1 %shard_map.139 = (f32[3,9945]{1,0:T(4,128)S(1)}, f32[3,9945]{1,0:T(4,128)S(1)}, f32[3,9945]{1,0:T(4,128)S(1)}) custom-call(f32[3,1,9945]{2,1,0:T(1,128)} %bitcast.19, f32[3,1,9945]{2,1,0:T(1,128)} %bitcast.20, f32[3,1,9945]{2,1,0:T(1,128)} %bitcast.21, s32[125,1,128]{2,1,0:T(1,128)} %bitcast.22, f32[9,125,1,128]{3,2,1,0:T(1,128)} %bitcast.18, ...), custom_call_target="tpu_custom_call" | custom-call | tf_op jit(solution)/shard_map/pallas_call | solution.py:525
  10.7 0.8 %shard_map.140 = (f32[3,1,9945]{2,1,0:T(1,128)}, f32[3,1,9945]{2,1,0:T(1,128)}, f32[3,1,9945]{2,1,0:T(1,128)}) custom-call(f32[3,9945]{1,0:T(4,128)S(1)} %get-tuple-element.9.pos, f32[3,9945]{1,0:T(4,128)S(1)} %get-tuple-element.10.vel, f32[3,9945]{1,0:T(4,128)S(1)} %get-tuple-element.11.acc), custom_call_target="tpu_custom_call" | custom-call | tf_op jit(solution)/shard_map/pallas_call | solution.py:579

commit v5 on v4

--- a/solution.py
+++ b/solution.py
@@ -80,10 +80,20 @@
     return np.stack([hi, low])
 
 
-def product(pair, y):
-    hi, low = split2(y)
+def product(hi, low, y):
+    top, rest = split2(y)
     dot = lambda a, b: jnp.dot(a, b, preferred_element_type=jnp.float32)
-    return dot(pair[0], hi) + dot(pair[0], low) + dot(pair[1], hi)
+    wide = lambda *parts: jnp.concatenate(parts, axis=1)
+    if y.shape[0] > 256:
+        first = dot(
+            wide(hi, hi, low),
+            jnp.concatenate([top[:, :256], rest[:, :256], top[:, :256]], axis=0),
+        )
+    else:
+        first = dot(hi, top[:, :256]) + dot(hi, rest[:, :256]) + dot(low, top[:, :256])
+    both = dot(hi, wide(top[:, 256:], rest[:, 256:]))
+    last = both[:, :128] + both[:, 128:] + dot(low, top[:, 256:])
+    return first[:, :128], first[:, 128:], last
 
 
 def ways():
@@ -162,10 +172,7 @@
         copies.append(pltpu.make_async_copy(src, dst, in_sem.at[6 + k]))
     for cp in copies:
         cp.start()
-    z_s[...] = jnp.zeros_like(z_s)
-    u_s[...] = jnp.zeros_like(u_s)
-    fl_s[...] = jnp.zeros_like(fl_s)
-    md_s[...] = jnp.zeros_like(md_s)
+    raw_s[:, 125:128, :] = jnp.zeros((13, 3, 128), jnp.float32)
     for ref in (m_recv, p_recv, q_recv, x_recv, e_recv, f_recv, c_recv):
         ref[...] = jnp.zeros_like(ref)
     copies[0].wait()
@@ -269,35 +276,32 @@
                 left, other, rise(turned)
             )
 
-    local = product(deriv_s, u_s[...])
-    grads = [
-        [local[l * 128 : l * 128 + 125, c * 128 : (c + 1) * 128] for c in range(3)]
-        for l in range(3)
-    ]
-    maps = [[sorted_s[3 * l + j, 0:125] for j in range(3)] for l in range(3)]
-    weight, lam, mu, dens_e = (sorted_s[9 + k, 0:125] for k in range(4))
-    h = [
-        [sum(grads[l][c] * maps[l][j] for l in range(3)) for j in range(3)] for c in range(3)
-    ]
-    div = lam * (h[0][0] + h[1][1] + h[2][2])
-    stress = [[None] * 3 for _ in range(3)]
-    for c in range(3):
-        for j in range(c, 3):
-            s = mu * (h[c][j] + h[j][c])
-            if c == j:
-                s = s + div
-            s = s * weight
-            stress[c][j] = s
-            stress[j][c] = s
-    for l in range(3):
+    local = product(deriv_s[0], deriv_s[1], u_s[...])
+    for i in range(16):
+        at = slice(8 * i, 8 * i + 8)
+        maps = [[sorted_s[3 * l + j, at] for j in range(3)] for l in range(3)]
+        weight, lam, mu, dens_e = (sorted_s[9 + k, at] for k in range(4))
+        grads = [[local[c][128 * l + 8 * i : 128 * l + 8 * i + 8] for c in range(3)] for l in range(3)]
+        h = [
+            [sum(grads[l][c] * maps[l][j] for l in range(3)) for j in range(3)]
+            for c in range(3)
+        ]
+        mu = mu * weight
+        div = lam * weight * (h[0][0] + h[1][1] + h[2][2])
+        stress = [[None] * 3 for _ in range(3)]
         for c in range(3):
-            fl_s[l * 128 : l * 128 + 125, c * 128 : (c + 1) * 128] = sum(
-                stress[c][j] * maps[l][j] for j in range(3)
-            )
-    md_s[0:125, :] = dens_e * weight
+            for j in range(c, 3):
+                s = mu * (h[c][j] + h[j][c])
+                stress[c][j] = stress[j][c] = s + div if c == j else s
+        for l in range(3):
+            for c in range(3):
+                fl_s[128 * l + 8 * i : 128 * l + 8 * i + 8, 128 * c : 128 * (c + 1)] = sum(
+                    stress[c][j] * maps[l][j] for j in range(3)
+                )
+        md_s[at, :] = dens_e * weight
     for cp in copies[10:]:
         cp.wait()
-    terms = product(back_s, fl_s[...])
+    terms = product(back_s[0], back_s[1], fl_s[...])
     heavy = sum(
         jnp.dot(spread_s[...], part, preferred_element_type=jnp.float32)
         for part in split2(md_s[...])
@@ -305,7 +309,7 @@
 
     def term(c, a):
         at = slice(SLOT * a, SLOT * (a + 1))
-        return terms[at, 128 * c : 128 * (c + 1)] if c < 3 else heavy[at]
+        return terms[c][at] if c < 3 else heavy[at]
 
     sink = lambda v: pltpu.roll(v, 4, 0)
     tail = jnp.zeros((128, 128 - SLOT), jnp.float32)
@@ -325,6 +329,92 @@
             for ey in range(EY):
                 first = ((k[0] * EY + ey) * 4 + k[1]) * EX
                 z_s[first : first + EX, :] = part[EX * ey : EX * (ey + 1)]
+    sides = (pl.ds(0, 4, stride=16), pl.ds(64, 4))
+    lanes = lax.broadcasted_iota(jnp.int32, (SROW, 128), 1)
+    lane8 = lax.broadcasted_iota(jnp.int32, (8, 128), 1)
+    far = CHUNKS - 1
+    for sy in range(2):
+        ey = (EY - 1) * sy
+        base = STRIDE * sy
+        crown = top_s[pl.ds(EX * ey + EX - 1, 4, stride=each), :]
+        rows = jnp.concatenate([z_s[pl.ds(16 * ey, 4, stride=16 * EY), :], crown], axis=0)
+        first = TAIL * (1 - sy)
+        got = pltpu.roll(rows, (first - base) % 128, 1)
+        got = jnp.where((lane8 >= first) & (lane8 < first + NZ), got, 0.0)
+        f_send[0, sy] = got[:4]
+        f_send[1, sy] = got[4:]
+        for sz in range(2):
+            got = pltpu.roll(rows, (first - base + (8 if sz == 0 else -8)) % 128, 1)
+            got = jnp.where(lane8 == first + (NZ - 1) * (1 - sz), got, 0.0)
+            c_send[0, sy, sz] = got[:4]
+            c_send[1, sy, sz] = got[4:]
+        parts = [z_s[pl.ds(16 * (c * EY + ey) + 8 * h, 8), :] for c in range(4) for h in range(2)]
+        parts.append(jnp.concatenate([crown, jnp.zeros((4, 128), jnp.float32)], axis=0))
+        packed = None
+        for i, part in enumerate(parts):
+            got = jnp.where((lane8 >= base) & (lane8 < base + NZ), part, 0.0)
+            shift = (PITCH * i - base) % 128
+            got = pltpu.roll(got, shift, 1) if shift else got
+            packed = got if packed is None else packed + got
+        p_send[sy] = packed
+        place = lax.rem(lane8, PITCH)
+        for sz in range(2):
+            got = jnp.where(place == (NZ - 1) * sz, packed, 0.0)
+            q_send[sy, sz] = pltpu.roll(got, 8 if sz == 0 else 128 - 8, 1)
+
+    def route(way):
+        sx, sy, sz = ((w + 1) // 2 for w in way)
+        ox, oy, oz = 1 - sx, 1 - sy, 1 - sz
+        dx, dy, dz = (w != 0 for w in way)
+        if dx and dy and dz:
+            return c_send.at[sx, sy, sz], c_recv.at[ox, oy, oz]
+        if dx and dy:
+            return f_send.at[sx, sy], f_recv.at[ox, oy]
+        if dx and dz:
+            return e_send.at[sx, sz], e_recv.at[ox, oz]
+        if dy and dz:
+            return q_send.at[sy, sz], q_recv.at[oy, oz]
+        if dx:
+            return x_send.at[sx], x_recv.at[ox]
+        if dy:
+            return p_send.at[sy], p_recv.at[oy]
+        return m_send.at[sz], m_recv.at[oz]
+
+    def copy(source, target, peer):
+        return pltpu.make_async_remote_copy(
+            src_ref=source,
+            dst_ref=target,
+            send_sem=send_sem.at[0],
+            recv_sem=recv_sem.at[0],
+            device_id=peer,
+            device_id_type=MESH,
+        )
+
+    def await_all(settle):
+        for (nx, ny, nz), here in classes():
+            count = nx * CHUNKS + nx * ny + nx * nz + nx * ny * nz
+            count += 2 * ny + 2 * ny * nz + nz * SROW // 4
+            whole = tally.at[pl.ds(0, count)]
+
+            @pl.when(here)
+            def _():
+                settle(copy(whole, whole, links[0][2]))
+
+    peers = sum(there.astype(jnp.int32) for way, there, peer in links)
+    pl.semaphore_wait(barrier, peers)
+    farthest = sorted(range(len(WAYS)), key=lambda k: -sum(map(abs, WAYS[k])))
+
+    def depart(chosen):
+        for k in farthest:
+            way, there, peer = links[k]
+            if chosen(way):
+
+                @pl.when(there)
+                def _():
+                    copy(*route(way), peer).start()
+
+    depart(lambda way: way[1] != 0)
+
     for c in range(5):
         first, many = (16 * c, 16) if c < 4 else (64, 8)
         sums = [None] * CHUNKS
@@ -347,103 +437,35 @@
         for j in range(CHUNKS):
             grid_s[j, first : first + many, :] = sums[j]
 
-    sides = (pl.ds(0, 4, stride=16), pl.ds(64, 4))
-    lanes = lax.broadcasted_iota(jnp.int32, (SROW, 128), 1)
-    far = CHUNKS - 1
-    edge = grid_s[far]
-    rims = (grid_s[0], pltpu.roll(edge, 128 - TAIL, 1))
-    lane8 = lax.broadcasted_iota(jnp.int32, (8, 128), 1)
     for side in range(2):
         for j in range(CHUNKS):
             x_send[side, j] = grid_s[j, sides[side], :]
-    for sy in range(2):
-        rows = jnp.concatenate([x_send[0, far * sy], x_send[1, far * sy]], axis=0)
-        shift, first = (TAIL, TAIL) if sy == 0 else (128 - TAIL, 0)
-        got = pltpu.roll(rows, shift, 1)
-        got = jnp.where((lane8 >= first) & (lane8 < first + NZ), got, 0.0)
-        f_send[0, sy] = got[:4]
-        f_send[1, sy] = got[4:]
-        for sz in range(2):
-            got = pltpu.roll(rows, (shift + (8 if sz == 0 else 128 - 8)) % 128, 1)
-            got = jnp.where(lane8 == first + (NZ - 1) * (1 - sz), got, 0.0)
-            c_send[0, sy, sz] = got[:4]
-            c_send[1, sy, sz] = got[4:]
-        packed = None
-        for i in range(SROW // 8):
-            got = jnp.where(lane8 < NZ, rims[sy][8 * i : 8 * i + 8], 0.0)
-            got = pltpu.roll(got, PITCH * i, 1) if i else got
-            packed = got if packed is None else packed + got
-        p_send[sy] = packed
-        place = lax.rem(lane8, PITCH)
-        for sz in range(2):
-            got = jnp.where(place == (NZ - 1) * sz, packed, 0.0)
-            q_send[sy, sz] = pltpu.roll(got, 8 if sz == 0 else 128 - 8, 1)
-
-    def route(way):
-        sx, sy, sz = ((w + 1) // 2 for w in way)
-        ox, oy, oz = 1 - sx, 1 - sy, 1 - sz
-        dx, dy, dz = (w != 0 for w in way)
-        if dx and dy and dz:
-            return c_send.at[sx, sy, sz], c_recv.at[ox, oy, oz]
-        if dx and dy:
-            return f_send.at[sx, sy], f_recv.at[ox, oy]
-        if dx and dz:
-            return e_send.at[sx, sz], e_recv.at[ox, oz]
-        if dy and dz:
-            return q_send.at[sy, sz], q_recv.at[oy, oz]
-        if dx:
-            return x_send.at[sx], x_recv.at[ox]
-        if dy:
-            return p_send.at[sy], p_recv.at[oy]
-        return m_send.at[sz], m_recv.at[oz]
-
-    def copy(source, target, peer):
-        return pltpu.make_async_remote_copy(
-            src_ref=source,
-            dst_ref=target,
-            send_sem=send_sem.at[0],
-            recv_sem=recv_sem.at[0],
-            device_id=peer,
-            device_id_type=MESH,
-        )
-
-    def await_all(settle):
-        for (nx, ny, nz), here in classes():
-            count = nx * CHUNKS + nx * ny + nx * nz + nx * ny * nz
-            count += 2 * ny + 2 * ny * nz + nz * SROW // 4
-            whole = tally.at[pl.ds(0, count)]
-
-            @pl.when(here)
-            def _():
-                settle(copy(whole, whole, links[0][2]))
-
-    peers = sum(there.astype(jnp.int32) for way, there, peer in links)
-    pl.semaphore_wait(barrier, peers)
-    farthest = sorted(range(len(WAYS)), key=lambda k: -sum(map(abs, WAYS[k])))
-
-    def depart(chosen):
-        for k in farthest:
-            way, there, peer = links[k]
-            if chosen(way):
-
-                @pl.when(there)
-                def _():
-                    copy(*route(way), peer).start()
-
-    flat = lambda way: way[1] == 0 and way[2] != 0
-    depart(lambda way: not flat(way))
-    for dz in range(2):
-        face = None
-        source = jnp.minimum(NZ * lanes + (NZ - 1) * dz, 128 * CHUNKS - 1)
+    sources = [
+        jnp.minimum(NZ * lanes + (NZ - 1) * dz, 128 * CHUNKS - 1) for dz in range(2)
+    ]
+
+    def face(parts, dz):
+        many = parts[0].shape[0]
+        source = sources[dz][:many]
+        found = None
         for j in range(CHUNKS):
             got = jnp.take_along_axis(
-                grid_s[j], source & 127, axis=1, mode="promise_in_bounds"
+                parts[j], source & 127, axis=1, mode="promise_in_bounds"
             )
-            face = got if face is None else jnp.where(source >= 128 * j, got, face)
-        m_send[dz] = jnp.where(lanes < NY, face, 0.0)
-        for side in range(2):
-            e_send[side, dz] = m_send[dz, sides[side], :]
-    depart(flat)
+            found = got if found is None else jnp.where(source >= 128 * j, got, found)
+        return jnp.where(lanes[:many] < NY, found, 0.0)
+
+    rims = [
+        jnp.concatenate([x_send[0, j], x_send[1, j]], axis=0) for j in range(CHUNKS)
+    ]
+    for dz in range(2):
+        got = face(rims, dz)
+        e_send[0, dz] = got[:4]
+        e_send[1, dz] = got[4:]
+    depart(lambda way: way[1] == 0 and way[0] != 0)
+    for dz in range(2):
+        m_send[dz] = face([grid_s[j] for j in range(CHUNKS)], dz)
+    depart(lambda way: way[1] == 0 and way[0] == 0)
     vel_out[...] = v_s[...] + half * a_s[...]
 
     await_all(lambda copied: copied.wait_recv())

time: 11.6 us -> 11.3 us (0.974)
  Pallas kernels: 10.8 us -> 10.5 us
    pallas_call x1, Pallas kernels: 10.1 us -> 9.78 us  [body(): pl.pallas_call(kernel, out_shape=[pltpu.VMEM((3, nodes), f32)] * 3, in_sp...]
where the time goes in v5:
time: 11.3 us; the launch traced here: 11.2 us
  Pallas kernels  10.5 us (93%)
  between operations  0.64 us (6%)
    pallas_call x1, Pallas kernels, body(): pl.pallas_call(kernel, out_shape=[pltpu.VMEM((3, nodes), f32)] * 3, in_sp...  9.78 us
    pallas_call x1, Pallas kernels, body(): pl.pallas_call(finish, out_shape=[out] * 3, in_specs=[vmem] * 3, out_spec...  0.76 us

profile of v5, /device:TPU:1, one launch (start us, length us, event | category | flops | bytes accessed | tf_op | source)
XLA Modules:
  0.0 11.2 jit_solution(11112854116176636514)
XLA Ops:
  0.6 9.8 %shard_map.139 = (f32[3,9945]{1,0:T(4,128)S(1)}, f32[3,9945]{1,0:T(4,128)S(1)}, f32[3,9945]{1,0:T(4,128)S(1)}) custom-call(f32[3,1,9945]{2,1,0:T(1,128)} %bitcast.19, f32[3,1,9945]{2,1,0:T(1,128)} %bitcast.20, f32[3,1,9945]{2,1,0:T(1,128)} %bitcast.21, s32[125,1,128]{2,1,0:T(1,128)} %bitcast.22, f32[9,125,1,128]{3,2,1,0:T(1,128)} %bitcast.18, ...), custom_call_target="tpu_custom_call" | custom-call | tf_op jit(solution)/shard_map/pallas_call | solution.py:547
  10.4 0.8 %shard_map.140 = (f32[3,1,9945]{2,1,0:T(1,128)}, f32[3,1,9945]{2,1,0:T(1,128)}, f32[3,1,9945]{2,1,0:T(1,128)}) custom-call(f32[3,9945]{1,0:T(4,128)S(1)} %get-tuple-element.9.pos, f32[3,9945]{1,0:T(4,128)S(1)} %get-tuple-element.10.vel, f32[3,9945]{1,0:T(4,128)S(1)} %get-tuple-element.11.acc), custom_call_target="tpu_custom_call" | custom-call | tf_op jit(solution)/shard_map/pallas_call | solution.py:601

commit v6 on v5

--- a/solution.py
+++ b/solution.py
@@ -315,7 +315,8 @@
     tail = jnp.zeros((128, 128 - SLOT), jnp.float32)
     crest = {}
     rows = lax.broadcasted_iota(jnp.int32, (each, 128), 0)
-    for (c, a), (d, b) in (((0, 4), (1, 4)), ((2, 4), (3, 4))) + PAIRS:
+    def settle_block(one_at, two_at):
+        (c, a), (d, b) = one_at, two_at
         one, two = term(c, a), term(d, b)
         both = jnp.where(left, one, sink(two)) + pltpu.roll(jnp.where(left, two, sink(one)), 64, 1)
         turned = jnp.concatenate([jnp.transpose(both), tail], axis=1)
@@ -329,39 +330,16 @@
             for ey in range(EY):
                 first = ((k[0] * EY + ey) * 4 + k[1]) * EX
                 z_s[first : first + EX, :] = part[EX * ey : EX * (ey + 1)]
+
+    def row_ends(sy):
+        ey = (EY - 1) * sy
+        crown = top_s[pl.ds(EX * ey + EX - 1, 4, stride=each), :]
+        return ey, STRIDE * sy, crown
+
     sides = (pl.ds(0, 4, stride=16), pl.ds(64, 4))
     lanes = lax.broadcasted_iota(jnp.int32, (SROW, 128), 1)
     lane8 = lax.broadcasted_iota(jnp.int32, (8, 128), 1)
     far = CHUNKS - 1
-    for sy in range(2):
-        ey = (EY - 1) * sy
-        base = STRIDE * sy
-        crown = top_s[pl.ds(EX * ey + EX - 1, 4, stride=each), :]
-        rows = jnp.concatenate([z_s[pl.ds(16 * ey, 4, stride=16 * EY), :], crown], axis=0)
-        first = TAIL * (1 - sy)
-        got = pltpu.roll(rows, (first - base) % 128, 1)
-        got = jnp.where((lane8 >= first) & (lane8 < first + NZ), got, 0.0)
-        f_send[0, sy] = got[:4]
-        f_send[1, sy] = got[4:]
-        for sz in range(2):
-            got = pltpu.roll(rows, (first - base + (8 if sz == 0 else -8)) % 128, 1)
-            got = jnp.where(lane8 == first + (NZ - 1) * (1 - sz), got, 0.0)
-            c_send[0, sy, sz] = got[:4]
-            c_send[1, sy, sz] = got[4:]
-        parts = [z_s[pl.ds(16 * (c * EY + ey) + 8 * h, 8), :] for c in range(4) for h in range(2)]
-        parts.append(jnp.concatenate([crown, jnp.zeros((4, 128), jnp.float32)], axis=0))
-        packed = None
-        for i, part in enumerate(parts):
-            got = jnp.where((lane8 >= base) & (lane8 < base + NZ), part, 0.0)
-            shift = (PITCH * i - base) % 128
-            got = pltpu.roll(got, shift, 1) if shift else got
-            packed = got if packed is None else packed + got
-        p_send[sy] = packed
-        place = lax.rem(lane8, PITCH)
-        for sz in range(2):
-            got = jnp.where(place == (NZ - 1) * sz, packed, 0.0)
-            q_send[sy, sz] = pltpu.roll(got, 8 if sz == 0 else 128 - 8, 1)
-
     def route(way):
         sx, sy, sz = ((w + 1) // 2 for w in way)
         ox, oy, oz = 1 - sx, 1 - sy, 1 - sz
@@ -401,19 +379,63 @@
                 settle(copy(whole, whole, links[0][2]))
 
     peers = sum(there.astype(jnp.int32) for way, there, peer in links)
+    farthest = sorted(range(len(WAYS)), key=lambda k: -sum(map(abs, WAYS[k])))
+
+    def depart(chosen):
+        for dy in (0, -1, 1):
+            leaving = [k for k in farthest if WAYS[k][1] == dy and chosen(WAYS[k])]
+
+            def send():
+                for k in leaving:
+                    way, there, peer = links[k]
+                    if way in ((0, -1, 0), (0, 1, 0)):
+                        copy(*route(way), peer).start()
+                        continue
+
+                    @pl.when(there)
+                    def _():
+                        copy(*route(way), peer).start()
+
+            if leaving and dy:
+                pl.when(links[WAYS.index((0, dy, 0))][1])(send)
+            elif leaving:
+                send()
+
+    for one_at, two_at in (((0, 4), (1, 4)), ((2, 4), (3, 4))) + PAIRS[::2] + PAIRS[1::2]:
+        settle_block(one_at, two_at)
+    for sy in range(2):
+        ey, base, crown = row_ends(sy)
+        rows = jnp.concatenate([z_s[pl.ds(16 * ey, 4, stride=16 * EY), :], crown], axis=0)
+        first = TAIL * (1 - sy)
+        got = pltpu.roll(rows, (first - base) % 128, 1)
+        got = jnp.where((lane8 >= first) & (lane8 < first + NZ), got, 0.0)
+        f_send[0, sy] = got[:4]
+        f_send[1, sy] = got[4:]
+        for sz in range(2):
+            got = pltpu.roll(rows, (first - base + (8 if sz == 0 else -8)) % 128, 1)
+            got = jnp.where(lane8 == first + (NZ - 1) * (1 - sz), got, 0.0)
+            c_send[0, sy, sz] = got[:4]
+            c_send[1, sy, sz] = got[4:]
     pl.semaphore_wait(barrier, peers)
-    farthest = sorted(range(len(WAYS)), key=lambda k: -sum(map(abs, WAYS[k])))
-
-    def depart(chosen):
-        for k in farthest:
-            way, there, peer = links[k]
-            if chosen(way):
-
-                @pl.when(there)
-                def _():
-                    copy(*route(way), peer).start()
-
-    depart(lambda way: way[1] != 0)
+    depart(lambda way: way[0] != 0 and way[1] != 0)
+    for sy in range(2):
+        ey, base, crown = row_ends(sy)
+        parts = [z_s[pl.ds(16 * (c * EY + ey) + 8 * h, 8), :] for c in range(4) for h in range(2)]
+        parts.append(jnp.concatenate([crown, jnp.zeros((4, 128), jnp.float32)], axis=0))
+
+        def pack(low, high, move):
+            packed = None
+            for i, part in enumerate(parts):
+                got = jnp.where((lane8 >= base + low) & (lane8 < base + high), part, 0.0)
+                shift = (PITCH * i - base + move) % 128
+                got = pltpu.roll(got, shift, 1) if shift else got
+                packed = got if packed is None else packed + got
+            return packed
+
+        p_send[sy] = pack(0, NZ, 0)
+        q_send[sy, 0] = pack(0, 1, NZ - 1)
+        q_send[sy, 1] = pack(NZ - 1, NZ, 1 - NZ)
+    depart(lambda way: way[0] == 0 and way[1] != 0)
 
     for c in range(5):
         first, many = (16 * c, 16) if c < 4 else (64, 8)

time: 11.3 us -> 11.2 us (level)
    pallas_call x1, Pallas kernels: 9.78 us -> 9.67 us  [body(): pl.pallas_call(kernel, out_shape=[pltpu.VMEM((3, nodes), f32)] * 3, in_sp...]
where the time goes in v6:
time: 11.2 us; the launch traced here: 11.1 us
  Pallas kernels  10.4 us (93%)
  between operations  0.64 us (6%)
    pallas_call x1, Pallas kernels, body(): pl.pallas_call(kernel, out_shape=[pltpu.VMEM((3, nodes), f32)] * 3, in_sp...  9.67 us
    pallas_call x1, Pallas kernels, body(): pl.pallas_call(finish, out_shape=[out] * 3, in_specs=[vmem] * 3, out_spec...  0.76 us

profile of v6, /device:TPU:1, one launch (start us, length us, event | category | flops | bytes accessed | tf_op | source)
XLA Modules:
  0.0 11.1 jit_solution(16978116571833229191)
XLA Ops:
  0.6 9.7 %shard_map.139 = (f32[3,9945]{1,0:T(4,128)S(1)}, f32[3,9945]{1,0:T(4,128)S(1)}, f32[3,9945]{1,0:T(4,128)S(1)}) custom-call(f32[3,1,9945]{2,1,0:T(1,128)} %bitcast.19, f32[3,1,9945]{2,1,0:T(1,128)} %bitcast.20, f32[3,1,9945]{2,1,0:T(1,128)} %bitcast.21, s32[125,1,128]{2,1,0:T(1,128)} %bitcast.22, f32[9,125,1,128]{3,2,1,0:T(1,128)} %bitcast.18, ...), custom_call_target="tpu_custom_call" | custom-call | tf_op jit(solution)/shard_map/pallas_call | solution.py:569
  10.3 0.8 %shard_map.140 = (f32[3,1,9945]{2,1,0:T(1,128)}, f32[3,1,9945]{2,1,0:T(1,128)}, f32[3,1,9945]{2,1,0:T(1,128)}) custom-call(f32[3,9945]{1,0:T(4,128)S(1)} %get-tuple-element.9.pos, f32[3,9945]{1,0:T(4,128)S(1)} %get-tuple-element.10.vel, f32[3,9945]{1,0:T(4,128)S(1)} %get-tuple-element.11.acc), custom_call_target="tpu_custom_call" | custom-call | tf_op jit(solution)/shard_map/pallas_call | solution.py:623

commit v7 on v6

--- a/solution.py
+++ b/solution.py
@@ -20,6 +20,7 @@
 SROW = 72
 TAIL = PLANE - NZ - 128 * (CHUNKS - 1)
 PITCH = 14
+ORDER = (4, 0, 1, 2, 3)
 SPLITS = ((0, 7), (7, 6))
 PAIRS = tuple(((c, a), (c, a + 1)) for c in range(4) for a in (0, 2))
 
@@ -65,7 +66,8 @@
         deriv[l * 128 : l * 128 + 125] = parts[l] @ pad
     spread = np.zeros((5 * SLOT, 128), np.float32)
     spread[:, :125] = pad.T
-    return deriv, -deriv.T.copy(), spread
+    rows = np.concatenate([np.arange(SLOT * a, SLOT * (a + 1)) for a in ORDER])
+    return deriv, -deriv.T[rows], spread[rows]
 
 
 def split2(x):
@@ -308,7 +310,7 @@
     )
 
     def term(c, a):
-        at = slice(SLOT * a, SLOT * (a + 1))
+        at = slice(SLOT * ORDER.index(a), SLOT * (ORDER.index(a) + 1))
         return terms[c][at] if c < 3 else heavy[at]
 
     sink = lambda v: pltpu.roll(v, 4, 0)

time: 11.2 us -> 11.2 us (level)
  no operation moved by 1% of the time
where the time goes in v7:
time: 11.2 us; the launch traced here: 11.1 us
  Pallas kernels  10.4 us (93%)
  between operations  0.64 us (6%)
    pallas_call x1, Pallas kernels, body(): pl.pallas_call(kernel, out_shape=[pltpu.VMEM((3, nodes), f32)] * 3, in_sp...  9.66 us
    pallas_call x1, Pallas kernels, body(): pl.pallas_call(finish, out_shape=[out] * 3, in_specs=[vmem] * 3, out_spec...  0.76 us

profile of v7, /device:TPU:1, one launch (start us, length us, event | category | flops | bytes accessed | tf_op | source)
XLA Modules:
  0.0 11.1 jit_solution(8837656243429684127)
XLA Ops:
  0.6 9.7 %shard_map.139 = (f32[3,9945]{1,0:T(4,128)S(1)}, f32[3,9945]{1,0:T(4,128)S(1)}, f32[3,9945]{1,0:T(4,128)S(1)}) custom-call(f32[3,1,9945]{2,1,0:T(1,128)} %bitcast.19, f32[3,1,9945]{2,1,0:T(1,128)} %bitcast.20, f32[3,1,9945]{2,1,0:T(1,128)} %bitcast.21, s32[125,1,128]{2,1,0:T(1,128)} %bitcast.22, f32[9,125,1,128]{3,2,1,0:T(1,128)} %bitcast.18, ...), custom_call_target="tpu_custom_call" | custom-call | tf_op jit(solution)/shard_map/pallas_call | solution.py:571
  10.3 0.8 %shard_map.140 = (f32[3,1,9945]{2,1,0:T(1,128)}, f32[3,1,9945]{2,1,0:T(1,128)}, f32[3,1,9945]{2,1,0:T(1,128)}) custom-call(f32[3,9945]{1,0:T(4,128)S(1)} %get-tuple-element.9.pos, f32[3,9945]{1,0:T(4,128)S(1)} %get-tuple-element.10.vel, f32[3,9945]{1,0:T(4,128)S(1)} %get-tuple-element.11.acc), custom_call_target="tpu_custom_call" | custom-call | tf_op jit(solution)/shard_map/pallas_call | solution.py:625

commit v8 on v7

--- a/solution.py
+++ b/solution.py
@@ -23,6 +23,7 @@
 ORDER = (4, 0, 1, 2, 3)
 SPLITS = ((0, 7), (7, 6))
 PAIRS = tuple(((c, a), (c, a + 1)) for c in range(4) for a in (0, 2))
+FIRST = (((0, 4), (1, 4)),) + PAIRS[:4:2] + (((2, 4), (3, 4)),) + PAIRS[4::2]
 
 LIMIT = 65 * 1000 * 1000
 
@@ -403,7 +404,7 @@
             elif leaving:
                 send()
 
-    for one_at, two_at in (((0, 4), (1, 4)), ((2, 4), (3, 4))) + PAIRS[::2] + PAIRS[1::2]:
+    for one_at, two_at in FIRST + PAIRS[1::2]:
         settle_block(one_at, two_at)
     for sy in range(2):
         ey, base, crown = row_ends(sy)

time: 11.2 us -> 11.2 us (level)
  no operation moved by 1% of the time
where the time goes in v8:
time: 11.2 us; the launch traced here: 11.1 us
  Pallas kernels  10.4 us (93%)
  between operations  0.64 us (6%)
    pallas_call x1, Pallas kernels, body(): pl.pallas_call(kernel, out_shape=[pltpu.VMEM((3, nodes), f32)] * 3, in_sp...  9.66 us
    pallas_call x1, Pallas kernels, body(): pl.pallas_call(finish, out_shape=[out] * 3, in_specs=[vmem] * 3, out_spec...  0.76 us

profile of v8, /device:TPU:1, one launch (start us, length us, event | category | flops | bytes accessed | tf_op | source)
XLA Modules:
  0.0 11.1 jit_solution(1913978182236257806)
XLA Ops:
  0.6 9.7 %shard_map.139 = (f32[3,9945]{1,0:T(4,128)S(1)}, f32[3,9945]{1,0:T(4,128)S(1)}, f32[3,9945]{1,0:T(4,128)S(1)}) custom-call(f32[3,1,9945]{2,1,0:T(1,128)} %bitcast.19, f32[3,1,9945]{2,1,0:T(1,128)} %bitcast.20, f32[3,1,9945]{2,1,0:T(1,128)} %bitcast.21, s32[125,1,128]{2,1,0:T(1,128)} %bitcast.22, f32[9,125,1,128]{3,2,1,0:T(1,128)} %bitcast.18, ...), custom_call_target="tpu_custom_call" | custom-call | tf_op jit(solution)/shard_map/pallas_call | solution.py:572
  10.3 0.8 %shard_map.140 = (f32[3,1,9945]{2,1,0:T(1,128)}, f32[3,1,9945]{2,1,0:T(1,128)}, f32[3,1,9945]{2,1,0:T(1,128)}) custom-call(f32[3,9945]{1,0:T(4,128)S(1)} %get-tuple-element.9.pos, f32[3,9945]{1,0:T(4,128)S(1)} %get-tuple-element.10.vel, f32[3,9945]{1,0:T(4,128)S(1)} %get-tuple-element.11.acc), custom_call_target="tpu_custom_call" | custom-call | tf_op jit(solution)/shard_map/pallas_call | solution.py:626
